TPU v7x, 32 devices: a whole 2x2x4 slice. The times are simulated.
32 devices in a mesh: grp: 8 (over z, core), dom: 4 (over y, x).
Axes of the slice: x: 2, y: 2, z: 4, core: 2. Of those that a mesh axis runs over, the one named last changes fastest.
Arguments:
- connect: int32 [20, 4096], P(None, ('grp', 'dom')), may hold values from 0 to 511, as said below
- interface_nodes: int32 [32, 4, 32], P(('grp', 'dom')), may hold values from 0 to 511, as said below
- neighbours: int32 [32, 4], P(('grp', 'dom')), may hold values from 0 to 1, as said below
- point_rank: int32 [32, 2048], P(('grp', 'dom')), may hold values from 0 to 2047, each once within a row
- shape_grad: float32 [48, 20], replicated, may hold values from -1.25 to 1.25
- inverse_jacobian: float32 [9, 4096], P(None, ('grp', 'dom')), may hold values from -0.45 to 2.5
- lame_moduli: float32 [2, 4096], P(None, ('grp', 'dom')), may hold values from 0.5 to 2
- point_weights: float32 [16, 4096], P(None, ('grp', 'dom')), may hold values from 0.003 to 0.02
- mass_elem: float32 [20, 4096], P(None, ('grp', 'dom')), may hold values from 0.5 to 2
- source_pattern: float32 [3, 16384], P(None, ('grp', 'dom')), may hold values from -6 to 6
- wavelet: float32 [16], replicated, may hold values from -6 to 6
Outputs:
- strain_db: bfloat16 [16, 6, 65536], P(None, None, ('grp', 'dom'))
Inputs may be any that keep to these rules, and one draw needn't show every extreme that they name: `connect`: every one of a partition's 512 nodes is named by some element of that partition. `interface_nodes`: entry i of list k of a partition and entry i of the opposite list of the partition beside it in direction k are copies of one node; no node stands twice among a partition's four lists. `neighbours`: the entry of a partition in direction k equals that of the partition beside it in the opposite direction; it is 0 where no partition lies in direction k.
All inputs are finite; a program needn't handle non-finite values.
Results may differ from a plain program's by a relative error of at most 0.001.
Values may be sent and summed in bfloat16 or wider, within the bound.
A program may use at most 64 MiB of HBM per device.

v0:
```python
import functools

import jax
import jax.numpy as jnp
from jax import lax
from jax.experimental import pallas as pl
from jax.experimental.pallas import tpu as pltpu
from jax.sharding import PartitionSpec as P

MESH = pl.DeviceIdType.MESH
F32 = jnp.float32
BF16 = jnp.bfloat16
time_step = 0.5
LANES = 128


def split(x):
    hi = x.astype(BF16)
    return hi, (x - hi.astype(F32)).astype(BF16)


def pick_lanes(x, idx):
    return jnp.take_along_axis(x, idx, axis=1, mode="promise_in_bounds")


def kernel(
    groups,
    writers,
    steps,
    nodes_el,
    conn_ref,
    faces_ref,
    nb_ref,
    rank_ref,
    gradt_ref,
    jac_ref,
    lame_ref,
    pw_ref,
    mass_ref,
    src_ref,
    wav_ref,
    out_ref,
    onehot,
    hmask,
    perm,
    w1,
    w2,
    snaps,
    lhs,
    ordered,
    send,
    recv,
    send_sem,
    recv_sem,
    out_send_sem,
    out_recv_sem,
):
    g = lax.axis_index("grp")
    d = lax.axis_index("dom")
    points = pw_ref.shape[0]
    block = out_ref.shape[2] // writers
    blocks = src_ref.shape[1] // LANES

    recv[...] = jnp.zeros_like(recv)
    has = (g > 0, g < groups - 1, d > 0, d < writers - 1)
    where_to = ((g - 1, d), (g + 1, d), (g, d - 1), (g, d + 1))

    barrier = pltpu.get_barrier_semaphore()
    for k in range(2):

        @pl.when(has[k])
        def _():
            pl.semaphore_signal(barrier, inc=1, device_id=where_to[k], device_id_type=MESH)

    for i in range(1, writers):
        pl.semaphore_signal(
            barrier, inc=1, device_id=(g, lax.rem(d + i, writers)), device_id_type=MESH
        )

    lane = lax.broadcasted_iota(jnp.int32, (LANES, LANES), 1)
    row16 = lax.broadcasted_iota(jnp.int32, (16, LANES), 0)
    faces = faces_ref[0].astype(F32)
    face_row = jnp.concatenate([faces[k : k + 1, :] for k in range(4)], axis=1)
    face_swap = jnp.concatenate([faces[k ^ 1 : (k ^ 1) + 1, :] for k in range(4)], axis=1)
    face_swap = face_swap.astype(jnp.int32)
    face_low = jnp.broadcast_to(jnp.bitwise_and(face_swap, LANES - 1), (8, LANES))
    face_mask = jnp.where(
        jnp.right_shift(face_swap, 7) == jnp.right_shift(row16, 2), 1.0, 0.0
    )
    face_col = jnp.broadcast_to(face_row, (LANES, LANES)).T
    position = lax.broadcasted_iota(jnp.int32, (LANES, LANES), 0).astype(F32)
    inv_rows = []
    has_rows = []
    for b in range(blocks):
        hit = jnp.where(face_col == (lane + b * LANES).astype(F32), 1.0, 0.0)
        inv_rows.append(
            jnp.broadcast_to(jnp.sum(hit * position, axis=0, keepdims=True), (4, LANES))
        )
        has_rows.append(jnp.broadcast_to(jnp.sum(hit, axis=0, keepdims=True), (4, LANES)))
    inv_idx = jnp.concatenate(inv_rows, axis=0).astype(jnp.int32)
    inv_has = jnp.concatenate(has_rows, axis=0)

    conn_low = jnp.bitwise_and(conn_ref[...], LANES - 1)
    conn_high = jnp.right_shift(conn_ref[...], 7)
    columns = jnp.concatenate(
        [conn_low.astype(F32), jnp.zeros((LANES - nodes_el, LANES), F32)], axis=0
    ).T
    for n in range(nodes_el):
        here = jnp.broadcast_to(columns[:, n : n + 1], (LANES, LANES))
        hit = jnp.where(here == lane.astype(F32), 1.0, 0.0)
        onehot[n * LANES : (n + 1) * LANES, 0:LANES] = hit.astype(BF16)
        hit = jnp.where(here == face_low[0:1, :].astype(F32), 1.0, 0.0)
        onehot[n * LANES : (n + 1) * LANES, LANES:] = hit.astype(BF16)
        hmask[n * 16 : (n + 1) * 16, :] = jnp.where(
            conn_high[n : n + 1, :] == jnp.right_shift(row16, 2), 1.0, 0.0
        ).astype(BF16)
    gradt = gradt_ref[...]
    depth = 3 * points
    hi = gradt.astype(BF16).astype(F32)
    lo = gradt - hi
    gap = jnp.zeros((32 - nodes_el, depth), F32)
    tall = jnp.concatenate([hi, gap, hi, gap, lo, gap, jnp.zeros((32, depth), F32)], axis=0)
    tall = jnp.concatenate([tall, jnp.zeros((LANES, LANES - depth), F32)], axis=1)
    w1[...] = tall.T[0:depth, 0:96].astype(BF16)
    wide = jnp.concatenate([hi] * 6 + [lo] * 3, axis=1)
    col = lax.broadcasted_iota(jnp.int32, (8, 9 * depth), 1)
    rows = jnp.bitwise_and(lax.broadcasted_iota(jnp.int32, (8, 9 * depth), 0), 3)
    own = (col >= rows * depth) & (col < (rows + 1) * depth)
    for piece in (3, 6):
        own = own | ((col >= (rows + piece) * depth) & (col < (rows + piece + 1) * depth))
    own = own & (rows < 3)
    for n in range(0, nodes_el, 2):
        two = [jnp.where(own, wide[m : m + 1, :], 0.0) for m in (n, n + 1)]
        w2[n * 8 : n * 8 + 16, :] = jnp.concatenate(two, axis=0).astype(BF16)

    quarter = jnp.right_shift(lax.broadcasted_iota(jnp.int32, (8, LANES), 1), 5)
    nb = nb_ref[...].astype(F32)
    recv_mask = [jnp.where(quarter == k, nb[:, k : k + 1], 0.0) for k in range(4)]

    def copies(slot):
        return [
            pltpu.make_async_remote_copy(
                src_ref=send.at[slot],
                dst_ref=recv.at[slot, k ^ 1],
                send_sem=send_sem.at[slot, k],
                recv_sem=recv_sem.at[slot, k ^ 1],
                device_id=where_to[k],
                device_id_type=MESH,
            )
            for k in range(4)
        ]

    def arrivals(slot):
        return [
            pltpu.make_async_remote_copy(
                src_ref=send.at[slot],
                dst_ref=recv.at[slot, k],
                send_sem=send_sem.at[slot, k],
                recv_sem=recv_sem.at[slot, k],
                device_id=where_to[k],
                device_id_type=MESH,
            )
            for k in range(4)
        ]

    def send_shared(field, slot):
        part = field[:, LANES:] * face_mask
        part = part[0:8] + part[8:16]
        send[slot] = part + pltpu.roll(part, 4, 0)
        for k, copy in enumerate(copies(slot)):

            @pl.when(has[k])
            def _():
                copy.start()

    def shared_sum(slot):
        for k, copy in enumerate(arrivals(slot)):

            @pl.when(has[k])
            def _():
                copy.wait_recv()
                copy.wait_send()

        got = recv[slot, 0] * recv_mask[0]
        for k in range(1, 4):
            got = got + recv[slot, k] * recv_mask[k]
        return got

    def at_nodes(got):
        added = jnp.concatenate(
            [pick_lanes(got, inv_idx[0:8]), pick_lanes(got, inv_idx[8:16])], axis=0
        )
        return added * inv_has

    def scatter(rows):
        pieces = []
        for n in range(nodes_el):
            v = rows(n)
            hi, lo = split(jnp.concatenate([v, v], axis=0))
            mask = hmask[n * 16 : (n + 1) * 16, :]
            pieces.append(jnp.concatenate([hi * mask, lo * mask], axis=0))
        res = jnp.dot(
            jnp.concatenate(pieces, axis=1), onehot[...], preferred_element_type=F32
        )
        return res[0:16] + res[16:32]

    row8 = lax.broadcasted_iota(jnp.int32, (8, LANES), 0)
    mass_row = jnp.bitwise_and(row8, 3) == 3
    mass = scatter(lambda n: jnp.where(mass_row, mass_ref[n : n + 1, :], 0.0))
    src_rows = []
    for b in range(blocks):
        src_rows.append(src_ref[:, b * LANES : (b + 1) * LANES])
        src_rows.append(jnp.zeros((1, LANES), F32))
    source_rows = jnp.concatenate(src_rows, axis=0)
    source_low = jnp.concatenate(
        [pick_lanes(source_rows[i : i + 8], face_low) for i in (0, 8)], axis=0
    )
    first = mass + jnp.concatenate([source_rows, source_low], axis=1)

    pl.semaphore_wait(
        barrier, has[0].astype(jnp.int32) + has[1].astype(jnp.int32) + writers - 1
    )
    send_shared(first, 0)

    rank_row = lax.broadcasted_iota(jnp.int32, (perm.shape[0], LANES), 0)

    def build_order(q):
        start = pl.multiple_of(q * LANES, LANES)
        perm[:, pl.ds(start, LANES)] = jnp.where(
            rank_ref[:, pl.ds(start, LANES)] == rank_row, 1.0, 0.0
        ).astype(BF16)

    half = steps // 2
    tables = -(-points // half)
    for q in range(min(tables, points)):
        build_order(q)

    first = first[:, 0:LANES] + at_nodes(shared_sum(0))
    axis_row = jnp.bitwise_and(row16, 3) < 3
    source = jnp.where(axis_row, first, 0.0)
    total = jnp.concatenate(
        [jnp.broadcast_to(first[4 * b + 3 : 4 * b + 4, :], (4, LANES)) for b in range(blocks)],
        axis=0,
    )
    half_inverse = jnp.where(axis_row, time_step / total, 0.0)

    spare = jnp.zeros((24 - nodes_el, LANES), jnp.int32)
    conn_low = jnp.concatenate([conn_low, spare], axis=0)
    conn_high = jnp.concatenate([conn_high, spare], axis=0)
    low = [conn_low[8 * i : 8 * i + 8, :] for i in range(3)]
    high = [conn_high[8 * i : 8 * i + 8, :] for i in range(3)]

    def at_elements(rows_of):
        out = []
        for i in range(3):
            acc = None
            for b in range(blocks):
                val = pick_lanes(jnp.broadcast_to(rows_of(b), (8, LANES)), low[i])
                acc = val if b == 0 else jnp.where(high[i] == b, val, acc)
            out.append(acc)
        return out

    inv_f = inv_idx.astype(F32)
    place = [x.astype(jnp.int32) for x in at_elements(lambda b: inv_f[4 * b : 4 * b + 1, :])]
    coef = (-time_step) * half_inverse * inv_has
    coef = at_elements(lambda b: coef[4 * b : 4 * b + 1, :])

    def gather(u):
        return tuple(
            tuple(at_elements(lambda b: u[4 * b + c : 4 * b + c + 1, :])) for c in range(3)
        )

    def corrected(values, got):
        out = []
        for c in range(3):
            row = jnp.broadcast_to(got[c : c + 1, :], (8, LANES))
            out.append(
                tuple(values[c][i] + pick_lanes(row, place[i]) * coef[i] for i in range(3))
            )
        return tuple(out)

    def gradient(values):
        sides = []
        for c in range(3):
            rows = list(values[c]) + [jnp.zeros((8, LANES), F32)]
            hi, lo = split(jnp.concatenate(rows, axis=0))
            sides.append(jnp.concatenate([hi, lo, hi], axis=0))
        along = jnp.dot(
            w1[...], jnp.concatenate(sides, axis=1), preferred_element_type=F32
        )
        tensor = []
        for c in range(3):
            ref_dir = [
                along[r * points : (r + 1) * points, c * LANES : (c + 1) * LANES]
                for r in range(3)
            ]
            tensor.append(
                [
                    ref_dir[0] * jac_ref[e : e + 1, :]
                    + ref_dir[1] * jac_ref[3 + e : 4 + e, :]
                    + ref_dir[2] * jac_ref[6 + e : 7 + e, :]
                    for e in range(3)
                ]
            )
        return tensor

    def internal_force(t):
        lam = lame_ref[0:1, :]
        mu = lame_ref[1:2, :]
        pressure = lam * (t[0][0] + t[1][1] + t[2][2])
        stress = [[None] * 3 for _ in range(3)]
        for c in range(3):
            for e in range(c, 3):
                s = mu * (t[c][e] + t[e][c])
                if c == e:
                    s = s + pressure
                stress[c][e] = s
                stress[e][c] = s
        weight = pw_ref[...]
        highs = []
        lows = []
        for c in range(3):
            for r in range(3):
                m = stress[c][0] * jac_ref[3 * r : 3 * r + 1, :]
                m = m + stress[c][1] * jac_ref[3 * r + 1 : 3 * r + 2, :]
                m = m + stress[c][2] * jac_ref[3 * r + 2 : 3 * r + 3, :]
                hi, lo = split(m * weight)
                highs.append(hi)
                lows.append(lo)
        side = jnp.concatenate(highs + lows + highs, axis=0)
        values = jnp.dot(w2[...], side, preferred_element_type=F32)
        return scatter(lambda n: values[8 * n : 8 * n + 8, :])

    def record(t, slot_index):
        comps = [
            t[0][0],
            t[1][1],
            t[2][2],
            0.5 * (t[1][2] + t[2][1]),
            0.5 * (t[0][2] + t[2][0]),
            0.5 * (t[0][1] + t[1][0]),
        ]
        for c, value in enumerate(comps):
            start = (slot_index // half) * 6 + c
            start = pl.multiple_of((start * half + lax.rem(slot_index, half)) * points, points)
            snaps[pl.ds(start, points), :] = value

    velocity = wav_ref[0] * source * half_inverse
    displace = time_step * velocity

    def order_for(w):
        start = pl.multiple_of(w * block, block)
        res = lax.dot_general(
            lhs[...],
            perm[pl.ds(start, block), :],
            (((1,), (1,)), ((), ())),
            preferred_element_type=F32,
        )
        return res.astype(BF16).reshape(6, half, block)

    def mine(i):
        return pl.ds(pl.multiple_of(i * block, block), block)

    def parcel(h, i, column, target):
        return pltpu.make_async_remote_copy(
            src_ref=ordered.at[h, i],
            dst_ref=out_ref.at[:, h * half : (h + 1) * half, mine(column)],
            send_sem=out_send_sem.at[h, i],
            recv_sem=out_recv_sem.at[h, i],
            device_id=(g, target),
            device_id_type=MESH,
        )

    def ship(h):
        count = 6 * half
        for q in range(points):
            lhs[:, q * LANES : (q + 1) * LANES] = snaps[
                pl.ds(h * count * points + q, count, stride=points), :
            ].astype(BF16)
        for i in range(1, writers):
            w = lax.rem(d + i, writers)
            ordered[h, i] = order_for(w)
            parcel(h, i, d, w).start()
        out_ref[:, h * half : (h + 1) * half, mine(d)] = order_for(d)

    def advance(t, state, extra):
        values, displace, velocity = state
        slot = lax.rem(t, 2)
        tensor = gradient(values)
        inner = internal_force(tensor)
        send_shared(inner, slot)
        velocity = velocity + half_inverse * (wav_ref[t] * source - inner[:, 0:LANES])
        displace = displace + time_step * velocity
        values = gather(displace)
        record(tensor, t - 1)
        extra(t)
        got = shared_sum(slot)
        values = corrected(values, got)
        change = half_inverse * at_nodes(got)
        return values, displace - time_step * change, velocity - change

    def early(t, state):
        def extra(t):
            for i in range(tables):
                build_order(jnp.minimum(t * tables + i, points - 1))

        return advance(t, state, extra)

    state = (gather(displace), displace, velocity)
    state = lax.fori_loop(1, half, early, state)
    state = advance(jnp.int32(half), state, lambda t: ship(0))
    state = lax.fori_loop(
        half + 1, steps, lambda t, held: advance(t, held, lambda t: None), state
    )
    record(gradient(state[0]), jnp.int32(steps - 1))
    ship(1)
    for h in range(2):
        for i in range(1, writers):
            origin = lax.rem(d - i + writers, writers)
            parcel(h, i, origin, origin).wait_recv()
            w = lax.rem(d + i, writers)
            parcel(h, i, d, w).wait_send()


def solution(mesh):
    groups, writers = mesh.shape["grp"], mesh.shape["dom"]

    def shards(
        connect,
        interface_nodes,
        neighbours,
        point_rank,
        shape_grad,
        inverse_jacobian,
        lame_moduli,
        point_weights,
        mass_elem,
        source_pattern,
        wavelet,
    ):
        nodes_el, elements = connect.shape
        points = point_weights.shape[0]
        point_count = point_rank.shape[1]
        steps = wavelet.shape[0]
        vmem = pl.BlockSpec(memory_space=pltpu.VMEM)
        smem = pl.BlockSpec(memory_space=pltpu.SMEM)
        ordered = pl.pallas_call(
            functools.partial(kernel, groups, writers, steps, nodes_el),
            out_shape=jax.ShapeDtypeStruct((6, steps, point_count), BF16),
            in_specs=[vmem] * 10 + [smem],
            out_specs=vmem,
            scratch_shapes=[
                pltpu.VMEM((nodes_el * LANES, 2 * LANES), BF16),
                pltpu.VMEM((nodes_el * 16, LANES), BF16),
                pltpu.VMEM((point_count, point_count), BF16),
                pltpu.VMEM((3 * points, 96), BF16),
                pltpu.VMEM((nodes_el * 8, 27 * points), BF16),
                pltpu.VMEM((steps * 6 * points, LANES), F32),
                pltpu.VMEM((steps // 2 * 6, point_count), BF16),
                pltpu.VMEM((2, writers, 6, steps // 2, point_count // writers), BF16),
                pltpu.VMEM((2, 8, LANES), F32),
                pltpu.VMEM((2, 4, 8, LANES), F32),
                pltpu.SemaphoreType.DMA((2, 4)),
                pltpu.SemaphoreType.DMA((2, 4)),
                pltpu.SemaphoreType.DMA((2, writers)),
                pltpu.SemaphoreType.DMA((2, writers)),
            ],
            compiler_params=pltpu.CompilerParams(
                collective_id=0, has_side_effects=True, vmem_limit_bytes=56 * 1024 * 1024
            ),
            name="window",
        )(
            connect,
            interface_nodes,
            neighbours,
            point_rank,
            shape_grad.T,
            inverse_jacobian,
            lame_moduli,
            point_weights,
            mass_elem,
            source_pattern,
            wavelet,
        )
        return ordered.transpose(1, 0, 2)

    placed = (
        P(None, ("grp", "dom")),
        P(("grp", "dom"), None, None),
        P(("grp", "dom"), None),
        P(("grp", "dom"), None),
        P(),
        P(None, ("grp", "dom")),
        P(None, ("grp", "dom")),
        P(None, ("grp", "dom")),
        P(None, ("grp", "dom")),
        P(None, ("grp", "dom")),
        P(),
    )
    return jax.shard_map(
        shards, mesh=mesh, in_specs=placed, out_specs=P(None, None, ("grp", "dom")), check_vma=False
    )
```

profile of v0, /device:TPU:0, one launch (start us, length us, event | category | flops | bytes accessed | tf_op | source)
XLA Modules:
  0.0 72.6 jit_solution(11076968477568259354)
XLA Ops:
  0.0 70.8 %window.1 = bf16[6,16,2048]{2,1,0:T(8,128)(2,1)} custom-call(s32[20,128]{1,0:T(8,128)} %conn_ref.1, s32[1,4,32]{2,1,0:T(4,128)} %faces_ref.1, s32[1,4]{1,0:T(1,128)} %nb_ref.1, s32[1,2048]{1,0:T(1,128)} %rank_ref.1, f32[20,48]{1,0:T(8,128)} %bitcast.3, f32[9,128]{1,0:T(8,128)} %jac_ref.1, f32[2,128]{1,0:T(2,128)} %lame_ref.1, f32[16,128]{1,0:T(8,128)} %pw_ref.1, ...), custom_call_target="tpu_custom_call" | custom-call | tf_op jit(solution)/shard_map/window/pallas_call | solution.py:447
  70.8 1.8 %copy.13 = bf16[16,6,2048]{2,0,1:T(8,128)(2,1)} copy(bf16[16,6,2048]{2,0,1:T(8,128)(2,1)} %bitcast.2) | data formatting | bytes 786432
where the time goes:
time: 72.8 us; the launch traced here: 72.6 us
  Pallas kernels  70.8 us (97%)
  local copies, waits for them, and re-layouts  1.77 us (2%)
    pallas_call x1, Pallas kernels, shards(): pl.pallas_call(functools.partial(kernel, groups, writers, steps, nodes_el...  70.8 us
    unnamed x1, local copies, waits for them, and re-layouts  1.77 us

commit v1 on v0

--- a/solution.py
+++ b/solution.py
@@ -28,18 +28,39 @@
     writers,
     steps,
     nodes_el,
+    conn_in,
+    faces_in,
+    nb_in,
+    rank_in,
+    jac_in,
+    lame_in,
+    pw_in,
+    mass_in,
+    src_in,
+    gradt_ref,
+    wav_ref,
+    out_ref,
     conn_ref,
     faces_ref,
     nb_ref,
     rank_ref,
-    gradt_ref,
     jac_ref,
     lame_ref,
     pw_ref,
     mass_ref,
     src_ref,
-    wav_ref,
-    out_ref,
+    conn_own,
+    faces_own,
+    nb_own,
+    rank_own,
+    jac_own,
+    lame_own,
+    pw_own,
+    mass_own,
+    src_own,
+    move_sem,
+    move_send_sem,
+    move_recv_sem,
     onehot,
     hmask,
     perm,
@@ -55,27 +76,118 @@
     out_send_sem,
     out_recv_sem,
 ):
-    g = lax.axis_index("grp")
-    d = lax.axis_index("dom")
+    my_g = lax.axis_index("grp")
+    my_d = lax.axis_index("dom")
     points = pw_ref.shape[0]
     block = out_ref.shape[2] // writers
     blocks = src_ref.shape[1] // LANES
 
+    def along(w):
+        if writers % 4:
+            return w
+        return w + lax.rem(w // 2, 2) * (1 - 2 * lax.rem(w, 2))
+
+    def across(g, w):
+        if groups % 2:
+            return g
+        return g + lax.rem(w, 2) * (1 - 2 * lax.rem(g, 2))
+
+    def host(g, w):
+        return across(g, w), along(w)
+
+    d = along(my_d)
+    g = across(my_g, d)
+    stays = (g == my_g) & (d == my_d)
+    moves = jnp.logical_not(stays)
+    other_core = g != my_g
+    target = host(my_g, my_d)
+
+    has = (g > 0, g < groups - 1, d > 0, d < writers - 1)
+    where_to = (host(g - 1, d), host(g + 1, d), host(g, d - 1), host(g, d + 1))
+
+    arrays = (
+        (conn_in, conn_own, conn_ref),
+        (mass_in, mass_own, mass_ref),
+        (faces_in, faces_own, faces_ref),
+        (nb_in, nb_own, nb_ref),
+        (src_in, src_own, src_ref),
+        (jac_in, jac_own, jac_ref),
+        (lame_in, lame_own, lame_ref),
+        (pw_in, pw_own, pw_ref),
+        (rank_in, rank_own, rank_ref),
+    )
+
+    def fetch(i, kept):
+        return pltpu.make_async_copy(
+            arrays[i][0], arrays[i][2 if kept else 1], move_sem.at[i]
+        )
+
+    def move(i):
+        return pltpu.make_async_remote_copy(
+            src_ref=arrays[i][1],
+            dst_ref=arrays[i][2],
+            send_sem=move_send_sem.at[i],
+            recv_sem=move_recv_sem.at[i],
+            device_id=target,
+            device_id_type=MESH,
+        )
+
+    @pl.when(stays)
+    def _():
+        for i in range(len(arrays)):
+            fetch(i, True).start()
+
     recv[...] = jnp.zeros_like(recv)
-    has = (g > 0, g < groups - 1, d > 0, d < writers - 1)
-    where_to = ((g - 1, d), (g + 1, d), (g, d - 1), (g, d + 1))
-
     barrier = pltpu.get_barrier_semaphore()
-    for k in range(2):
+
+    @pl.when(moves)
+    def _():
+        for i in range(len(arrays)):
+            fetch(i, False).start()
+        pl.semaphore_signal(barrier, inc=1, device_id=(g, d), device_id_type=MESH)
+
+    for k in range(4):
 
         @pl.when(has[k])
         def _():
             pl.semaphore_signal(barrier, inc=1, device_id=where_to[k], device_id_type=MESH)
 
-    for i in range(1, writers):
-        pl.semaphore_signal(
-            barrier, inc=1, device_id=(g, lax.rem(d + i, writers)), device_id_type=MESH
-        )
+    for i in range(writers):
+        origin_d = lax.rem(my_d + i, writers)
+        origin = (across(my_g, along(origin_d)), origin_d)
+
+        def greet():
+            pl.semaphore_signal(barrier, inc=1, device_id=origin, device_id_type=MESH)
+
+        if i:
+            greet()
+        else:
+            pl.when(other_core)(greet)
+
+    expected = moves.astype(jnp.int32) + other_core.astype(jnp.int32) + writers - 1
+    for k in range(4):
+        expected = expected + has[k].astype(jnp.int32)
+    pl.semaphore_wait(barrier, expected)
+
+    @pl.when(moves)
+    def _():
+        for i in range(len(arrays)):
+            fetch(i, False).wait()
+            move(i).start()
+
+    def landed(lo, hi):
+        @pl.when(stays)
+        def _():
+            for i in range(lo, hi):
+                fetch(i, True).wait()
+
+        @pl.when(moves)
+        def _():
+            for i in range(lo, hi):
+                move(i).wait_recv()
+                move(i).wait_send()
+
+    landed(0, 5)
 
     lane = lax.broadcasted_iota(jnp.int32, (LANES, LANES), 1)
     row16 = lax.broadcasted_iota(jnp.int32, (16, LANES), 0)
@@ -217,10 +329,8 @@
     )
     first = mass + jnp.concatenate([source_rows, source_low], axis=1)
 
-    pl.semaphore_wait(
-        barrier, has[0].astype(jnp.int32) + has[1].astype(jnp.int32) + writers - 1
-    )
     send_shared(first, 0)
+    landed(5, len(arrays))
 
     rank_row = lax.broadcasted_iota(jnp.int32, (perm.shape[0], LANES), 0)
 
@@ -371,6 +481,10 @@
             device_id_type=MESH,
         )
 
+    def arriving(h, i):
+        origin = lax.rem(my_d - i + writers, writers)
+        return parcel(h, i, along(origin), origin)
+
     def ship(h):
         count = 6 * half
         for q in range(points):
@@ -378,10 +492,19 @@
                 pl.ds(h * count * points + q, count, stride=points), :
             ].astype(BF16)
         for i in range(1, writers):
-            w = lax.rem(d + i, writers)
+            w = lax.rem(my_d + i, writers)
             ordered[h, i] = order_for(w)
             parcel(h, i, d, w).start()
-        out_ref[:, h * half : (h + 1) * half, mine(d)] = order_for(d)
+        last = order_for(my_d)
+
+        @pl.when(other_core)
+        def _():
+            ordered[h, 0] = last
+            parcel(h, 0, d, my_d).start()
+
+        @pl.when(jnp.logical_not(other_core))
+        def _():
+            out_ref[:, h * half : (h + 1) * half, mine(d)] = last
 
     def advance(t, state, extra):
         values, displace, velocity = state
@@ -416,10 +539,13 @@
     ship(1)
     for h in range(2):
         for i in range(1, writers):
-            origin = lax.rem(d - i + writers, writers)
-            parcel(h, i, origin, origin).wait_recv()
-            w = lax.rem(d + i, writers)
-            parcel(h, i, d, w).wait_send()
+            arriving(h, i).wait_recv()
+            parcel(h, i, d, lax.rem(my_d + i, writers)).wait_send()
+
+        @pl.when(other_core)
+        def _():
+            arriving(h, 0).wait_recv()
+            parcel(h, 0, d, my_d).wait_send()
 
 
 def solution(mesh):
@@ -444,12 +570,26 @@
         steps = wavelet.shape[0]
         vmem = pl.BlockSpec(memory_space=pltpu.VMEM)
         smem = pl.BlockSpec(memory_space=pltpu.SMEM)
+        hbm = pl.BlockSpec(memory_space=pl.ANY)
+        sharded = (
+            connect,
+            interface_nodes,
+            neighbours,
+            point_rank,
+            inverse_jacobian,
+            lame_moduli,
+            point_weights,
+            mass_elem,
+            source_pattern,
+        )
         ordered = pl.pallas_call(
             functools.partial(kernel, groups, writers, steps, nodes_el),
             out_shape=jax.ShapeDtypeStruct((6, steps, point_count), BF16),
-            in_specs=[vmem] * 10 + [smem],
+            in_specs=[hbm] * len(sharded) + [vmem, smem],
             out_specs=vmem,
-            scratch_shapes=[
+            scratch_shapes=[pltpu.VMEM(a.shape, a.dtype) for a in sharded] * 2
+            + [pltpu.SemaphoreType.DMA((len(sharded),))] * 3
+            + [
                 pltpu.VMEM((nodes_el * LANES, 2 * LANES), BF16),
                 pltpu.VMEM((nodes_el * 16, LANES), BF16),
                 pltpu.VMEM((point_count, point_count), BF16),
@@ -470,16 +610,8 @@
             ),
             name="window",
         )(
-            connect,
-            interface_nodes,
-            neighbours,
-            point_rank,
+            *sharded,
             shape_grad.T,
-            inverse_jacobian,
-            lame_moduli,
-            point_weights,
-            mass_elem,
-            source_pattern,
             wavelet,
         )
         return ordered.transpose(1, 0, 2)

time: 72.8 us -> 63.8 us (0.88)
  Pallas kernels: 70.8 us -> 61.5 us
    pallas_call x1, Pallas kernels: 70.8 us -> 61.5 us  [shards(): pl.pallas_call(functools.partial(kernel, groups, writers, steps, nodes_el...]
where the time goes in v1:
time: 63.8 us; the launch traced here: 63.2 us
  Pallas kernels  61.5 us (96%)
  local copies, waits for them, and re-layouts  1.77 us (3%)
    pallas_call x1, Pallas kernels, shards(): pl.pallas_call(functools.partial(kernel, groups, writers, steps, nodes_el...  61.5 us
    unnamed x1, local copies, waits for them, and re-layouts  1.77 us

profile of v1, /device:TPU:0, one launch (start us, length us, event | category | flops | bytes accessed | tf_op | source)
XLA Modules:
  0.0 63.2 jit_solution(6092789879733164973)
XLA Ops:
  0.0 61.5 %window.1 = bf16[6,16,2048]{2,1,0:T(8,128)(2,1)} custom-call(s32[20,128]{1,0:T(8,128)} %conn_in.1, s32[1,4,32]{2,1,0:T(4,128)} %faces_in.1, s32[1,4]{1,0:T(1,128)} %nb_in.1, s32[1,2048]{1,0:T(1,128)} %rank_in.1, f32[9,128]{1,0:T(8,128)} %jac_in.1, f32[2,128]{1,0:T(2,128)} %lame_in.1, f32[16,128]{1,0:T(8,128)} %pw_in.1, f32[20,128]{1,0:T(8,128)} %mass_in.1, ...), custom_call_target="tpu_custom_call" | custom-call | tf_op jit(solution)/shard_map/window/pallas_call | solution.py:585
  61.5 1.8 %copy.13 = bf16[16,6,2048]{2,0,1:T(8,128)(2,1)} copy(bf16[16,6,2048]{2,0,1:T(8,128)(2,1)} %bitcast.2) | data formatting | bytes 786432

commit v2 on v1

--- a/solution.py
+++ b/solution.py
@@ -61,11 +61,16 @@
     move_sem,
     move_send_sem,
     move_recv_sem,
-    onehot,
+    at_face,
+    at_node,
     hmask,
+    basis,
+    products,
+    pww,
+    kmat,
+    at_el,
     perm,
     w1,
-    w2,
     snaps,
     lhs,
     ordered,
@@ -187,18 +192,200 @@
                 move(i).wait_recv()
                 move(i).wait_send()
 
+
+    lane = lax.broadcasted_iota(jnp.int32, (LANES, LANES), 1)
+    row8 = lax.broadcasted_iota(jnp.int32, (8, LANES), 0)
+    row16 = lax.broadcasted_iota(jnp.int32, (16, LANES), 0)
+    pairs_el = nodes_el // 2
+    padded = -(-nodes_el // 8) * 8
+    tiles = padded // 8
+
+    gradt = gradt_ref[...]
+    depth = 3 * points
+    hi = gradt.astype(BF16).astype(F32)
+    lo = gradt - hi
+    gap = jnp.zeros((32 - nodes_el, depth), F32)
+    tall = jnp.concatenate([hi, gap, hi, gap, lo, gap, jnp.zeros((32, depth), F32)], axis=0)
+    tall = jnp.concatenate([tall, jnp.zeros((LANES, LANES - depth), F32)], axis=1)
+    w1[...] = tall.T[0:depth, 0:96].astype(BF16)
+
+    lanes = lax.broadcasted_iota(jnp.int32, (padded, LANES), 1)
+    base = jnp.concatenate([gradt, jnp.zeros((padded - nodes_el, depth), F32)], axis=0)
+    base = jnp.concatenate([base, jnp.zeros((padded, LANES - depth), F32)], axis=1)
+    own_dir = []
+    for r in range(3):
+        x = pltpu.roll(base, LANES - r * points, 1) if r else base
+        x = jnp.where(lanes < points, x, 0.0)
+        x = x + pltpu.roll(x, points, 1) + pltpu.roll(x, 2 * points, 1)
+        own_dir.append(x)
+        basis[r] = x
+
+    def multiply_pairs(m, carry):
+        for rp in range(3):
+            parts = []
+            for p in range(2):
+                other = basis[rp, pl.ds(2 * m + p, 1), :]
+                for r in range(3):
+                    product = own_dir[r] * other
+                    high = product.astype(BF16).astype(F32)
+                    parts.append(jnp.where(lanes < 2 * points, high, product - high))
+            rows = 6 * padded
+            products[m, rp * rows : (rp + 1) * rows, :] = jnp.concatenate(
+                parts, axis=0
+            ).astype(BF16)
+        return carry
+
+    lax.fori_loop(0, pairs_el, multiply_pairs, 0)
+
+    def clear(m, carry):
+        kmat[m] = jnp.zeros(kmat.shape[1:], F32)
+        return carry
+
+    lax.fori_loop(0, pairs_el, clear, 0)
+
     landed(0, 5)
-
-    lane = lax.broadcasted_iota(jnp.int32, (LANES, LANES), 1)
-    row16 = lax.broadcasted_iota(jnp.int32, (16, LANES), 0)
     faces = faces_ref[0].astype(F32)
     face_row = jnp.concatenate([faces[k : k + 1, :] for k in range(4)], axis=1)
     face_swap = jnp.concatenate([faces[k ^ 1 : (k ^ 1) + 1, :] for k in range(4)], axis=1)
-    face_swap = face_swap.astype(jnp.int32)
-    face_low = jnp.broadcast_to(jnp.bitwise_and(face_swap, LANES - 1), (8, LANES))
-    face_mask = jnp.where(
-        jnp.right_shift(face_swap, 7) == jnp.right_shift(row16, 2), 1.0, 0.0
-    )
+    face_swap = jnp.broadcast_to(face_swap.astype(jnp.int32), (LANES, LANES))
+    face_low = jnp.bitwise_and(face_swap[0:8], LANES - 1)
+    face_high = jnp.right_shift(face_swap[0:8], 7)
+
+    columns = jnp.concatenate(
+        [conn_ref[...].astype(F32), jnp.zeros((LANES - nodes_el, LANES), F32)], axis=0
+    ).T.astype(jnp.int32)
+
+    def column(n):
+        return jnp.broadcast_to(columns[:, n : n + 1], (LANES, LANES))
+
+    def spot(n):
+        j, p = n // 2, n % 2
+        return slice(j * LANES, (j + 1) * LANES), slice(p * LANES, (p + 1) * LANES)
+
+    for n in range(nodes_el):
+        at_face[spot(n)] = jnp.where(column(n) == face_swap, 1.0, 0.0).astype(BF16)
+
+    def pack(x):
+        high = x.astype(BF16).astype(F32)
+        return jnp.concatenate([high, x - high], axis=0).astype(BF16)
+
+    def face_forces(packs):
+        res = jnp.dot(
+            jnp.concatenate(packs, axis=1), at_face[...], preferred_element_type=F32
+        )
+        res = res[0:8] + res[8:16]
+        mixed = jnp.where(row8 < 4, res[:, 0:LANES], res[:, LANES:])
+        return mixed + pltpu.roll(mixed, 4, 0)
+
+    def node_forces(packs):
+        sides = []
+        for b in range(blocks):
+            sides.append(
+                jnp.concatenate(
+                    [
+                        packs[j] * hmask[(j * blocks + b) * 16 : (j * blocks + b + 1) * 16, :]
+                        for j in range(pairs_el)
+                    ],
+                    axis=1,
+                )
+            )
+        res = jnp.dot(
+            jnp.concatenate(sides, axis=0), at_node[...], preferred_element_type=F32
+        )
+        halves = []
+        for b in range(blocks):
+            one = res[16 * b : 16 * b + 8] + res[16 * b + 8 : 16 * b + 16]
+            even, odd = one[:, 0:LANES], one[:, LANES:]
+            if b % 2:
+                halves.append(pltpu.roll(even, 4, 0) + odd)
+            else:
+                halves.append(even + pltpu.roll(odd, 4, 0))
+        return jnp.concatenate(
+            [jnp.where(row8 < 4, halves[b], halves[b + 1]) for b in range(0, blocks, 2)],
+            axis=0,
+        )
+
+    quarter = jnp.right_shift(lax.broadcasted_iota(jnp.int32, (8, LANES), 1), 5)
+    nb = nb_ref[...].astype(F32)
+    recv_mask = [jnp.where(quarter == k, nb[:, k : k + 1], 0.0) for k in range(4)]
+
+    def copies(slot):
+        return [
+            pltpu.make_async_remote_copy(
+                src_ref=send.at[slot, 0:4],
+                dst_ref=recv.at[slot, k ^ 1, 0:4],
+                send_sem=send_sem.at[slot, k],
+                recv_sem=recv_sem.at[slot, k ^ 1],
+                device_id=where_to[k],
+                device_id_type=MESH,
+            )
+            for k in range(4)
+        ]
+
+    def arrivals(slot):
+        return [
+            pltpu.make_async_remote_copy(
+                src_ref=send.at[slot, 0:4],
+                dst_ref=recv.at[slot, k, 0:4],
+                send_sem=send_sem.at[slot, k],
+                recv_sem=recv_sem.at[slot, k],
+                device_id=where_to[k],
+                device_id_type=MESH,
+            )
+            for k in range(4)
+        ]
+
+    def send_shared(message, slot):
+        send[slot] = message
+        for k, copy in enumerate(copies(slot)):
+
+            @pl.when(has[k])
+            def _():
+                copy.start()
+
+    def shared_sum(slot):
+        for k, copy in enumerate(arrivals(slot)):
+
+            @pl.when(has[k])
+            def _():
+                copy.wait_recv()
+                copy.wait_send()
+
+        got = recv[slot, 0] * recv_mask[0]
+        for k in range(1, 4):
+            got = got + recv[slot, k] * recv_mask[k]
+        return got
+
+    masses = []
+    for n in range(0, nodes_el, 2):
+        mass = jnp.where(row8 == 3, mass_ref[n : n + 1, :], 0.0)
+        masses.append(pack(mass + jnp.where(row8 == 7, mass_ref[n + 1 : n + 2, :], 0.0)))
+    src_rows = []
+    for b in range(blocks):
+        src_rows.append(src_ref[:, b * LANES : (b + 1) * LANES])
+        src_rows.append(jnp.zeros((1, LANES), F32))
+    at_faces = jnp.zeros((8, LANES), F32)
+    for b in range(blocks):
+        rows = jnp.concatenate([src_rows[2 * b], jnp.zeros((5, LANES), F32)], axis=0)
+        at_faces = jnp.where(face_high == b, pick_lanes(rows, face_low), at_faces)
+    send_shared(face_forces(masses) + at_faces, 0)
+
+    conn_low = jnp.bitwise_and(conn_ref[...], LANES - 1)
+    conn_high = jnp.right_shift(conn_ref[...], 7)
+    for n in range(nodes_el):
+        low_column = jnp.bitwise_and(column(n), LANES - 1)
+        at_node[spot(n)] = jnp.where(low_column == lane, 1.0, 0.0).astype(BF16)
+    for j in range(pairs_el):
+        two = [
+            jnp.broadcast_to(conn_high[n : n + 1, :], (4, LANES)) for n in (2 * j, 2 * j + 1)
+        ]
+        two = jnp.concatenate(two * 2, axis=0)
+        for b in range(blocks):
+            hmask[(j * blocks + b) * 16 : (j * blocks + b + 1) * 16, :] = jnp.where(
+                two == b, 1.0, 0.0
+            ).astype(BF16)
+    first = node_forces(masses) + jnp.concatenate(src_rows, axis=0)
+
     face_col = jnp.broadcast_to(face_row, (LANES, LANES)).T
     position = lax.broadcasted_iota(jnp.int32, (LANES, LANES), 0).astype(F32)
     inv_rows = []
@@ -212,125 +399,57 @@
     inv_idx = jnp.concatenate(inv_rows, axis=0).astype(jnp.int32)
     inv_has = jnp.concatenate(has_rows, axis=0)
 
-    conn_low = jnp.bitwise_and(conn_ref[...], LANES - 1)
-    conn_high = jnp.right_shift(conn_ref[...], 7)
-    columns = jnp.concatenate(
-        [conn_low.astype(F32), jnp.zeros((LANES - nodes_el, LANES), F32)], axis=0
-    ).T
-    for n in range(nodes_el):
-        here = jnp.broadcast_to(columns[:, n : n + 1], (LANES, LANES))
-        hit = jnp.where(here == lane.astype(F32), 1.0, 0.0)
-        onehot[n * LANES : (n + 1) * LANES, 0:LANES] = hit.astype(BF16)
-        hit = jnp.where(here == face_low[0:1, :].astype(F32), 1.0, 0.0)
-        onehot[n * LANES : (n + 1) * LANES, LANES:] = hit.astype(BF16)
-        hmask[n * 16 : (n + 1) * 16, :] = jnp.where(
-            conn_high[n : n + 1, :] == jnp.right_shift(row16, 2), 1.0, 0.0
-        ).astype(BF16)
-    gradt = gradt_ref[...]
-    depth = 3 * points
-    hi = gradt.astype(BF16).astype(F32)
-    lo = gradt - hi
-    gap = jnp.zeros((32 - nodes_el, depth), F32)
-    tall = jnp.concatenate([hi, gap, hi, gap, lo, gap, jnp.zeros((32, depth), F32)], axis=0)
-    tall = jnp.concatenate([tall, jnp.zeros((LANES, LANES - depth), F32)], axis=1)
-    w1[...] = tall.T[0:depth, 0:96].astype(BF16)
-    wide = jnp.concatenate([hi] * 6 + [lo] * 3, axis=1)
-    col = lax.broadcasted_iota(jnp.int32, (8, 9 * depth), 1)
-    rows = jnp.bitwise_and(lax.broadcasted_iota(jnp.int32, (8, 9 * depth), 0), 3)
-    own = (col >= rows * depth) & (col < (rows + 1) * depth)
-    for piece in (3, 6):
-        own = own | ((col >= (rows + piece) * depth) & (col < (rows + piece + 1) * depth))
-    own = own & (rows < 3)
-    for n in range(0, nodes_el, 2):
-        two = [jnp.where(own, wide[m : m + 1, :], 0.0) for m in (n, n + 1)]
-        w2[n * 8 : n * 8 + 16, :] = jnp.concatenate(two, axis=0).astype(BF16)
-
-    quarter = jnp.right_shift(lax.broadcasted_iota(jnp.int32, (8, LANES), 1), 5)
-    nb = nb_ref[...].astype(F32)
-    recv_mask = [jnp.where(quarter == k, nb[:, k : k + 1], 0.0) for k in range(4)]
-
-    def copies(slot):
-        return [
-            pltpu.make_async_remote_copy(
-                src_ref=send.at[slot],
-                dst_ref=recv.at[slot, k ^ 1],
-                send_sem=send_sem.at[slot, k],
-                recv_sem=recv_sem.at[slot, k ^ 1],
-                device_id=where_to[k],
-                device_id_type=MESH,
-            )
-            for k in range(4)
-        ]
-
-    def arrivals(slot):
-        return [
-            pltpu.make_async_remote_copy(
-                src_ref=send.at[slot],
-                dst_ref=recv.at[slot, k],
-                send_sem=send_sem.at[slot, k],
-                recv_sem=recv_sem.at[slot, k],
-                device_id=where_to[k],
-                device_id_type=MESH,
-            )
-            for k in range(4)
-        ]
-
-    def send_shared(field, slot):
-        part = field[:, LANES:] * face_mask
-        part = part[0:8] + part[8:16]
-        send[slot] = part + pltpu.roll(part, 4, 0)
-        for k, copy in enumerate(copies(slot)):
-
-            @pl.when(has[k])
-            def _():
-                copy.start()
-
-    def shared_sum(slot):
-        for k, copy in enumerate(arrivals(slot)):
-
-            @pl.when(has[k])
-            def _():
-                copy.wait_recv()
-                copy.wait_send()
-
-        got = recv[slot, 0] * recv_mask[0]
-        for k in range(1, 4):
-            got = got + recv[slot, k] * recv_mask[k]
-        return got
-
     def at_nodes(got):
+        got = got + pltpu.roll(got, 4, 0)
         added = jnp.concatenate(
             [pick_lanes(got, inv_idx[0:8]), pick_lanes(got, inv_idx[8:16])], axis=0
         )
         return added * inv_has
 
-    def scatter(rows):
-        pieces = []
-        for n in range(nodes_el):
-            v = rows(n)
-            hi, lo = split(jnp.concatenate([v, v], axis=0))
-            mask = hmask[n * 16 : (n + 1) * 16, :]
-            pieces.append(jnp.concatenate([hi * mask, lo * mask], axis=0))
-        res = jnp.dot(
-            jnp.concatenate(pieces, axis=1), onehot[...], preferred_element_type=F32
-        )
-        return res[0:16] + res[16:32]
-
-    row8 = lax.broadcasted_iota(jnp.int32, (8, LANES), 0)
-    mass_row = jnp.bitwise_and(row8, 3) == 3
-    mass = scatter(lambda n: jnp.where(mass_row, mass_ref[n : n + 1, :], 0.0))
-    src_rows = []
-    for b in range(blocks):
-        src_rows.append(src_ref[:, b * LANES : (b + 1) * LANES])
-        src_rows.append(jnp.zeros((1, LANES), F32))
-    source_rows = jnp.concatenate(src_rows, axis=0)
-    source_low = jnp.concatenate(
-        [pick_lanes(source_rows[i : i + 8], face_low) for i in (0, 8)], axis=0
-    )
-    first = mass + jnp.concatenate([source_rows, source_low], axis=1)
-
-    send_shared(first, 0)
     landed(5, len(arrays))
+    weight = pw_ref[...]
+    hi = weight.astype(BF16).astype(F32)
+    pww[...] = jnp.concatenate(
+        [hi, weight - hi, hi, jnp.zeros((LANES - depth, LANES), F32)], axis=0
+    ).astype(BF16)
+    jac = [jnp.broadcast_to(jac_ref[i : i + 1, :], (8, LANES)) for i in range(9)]
+    lam = jnp.broadcast_to(lame_ref[0:1, :], (8, LANES))
+    mu = jnp.broadcast_to(lame_ref[1:2, :], (8, LANES))
+
+    def form_stiffness(m, carry):
+        moments = jnp.dot(products[m], pww[...], preferred_element_type=F32)
+        for p in range(2):
+            for i in range(tiles):
+
+                def moment(r, rp):
+                    start = ((rp * 2 + p) * 3 + r) * padded + 8 * i
+                    return moments[start : start + 8]
+
+                half = [
+                    [
+                        jac[a] * moment(0, rp) + jac[3 + a] * moment(1, rp) + jac[6 + a] * moment(2, rp)
+                        for rp in range(3)
+                    ]
+                    for a in range(3)
+                ]
+                full = [
+                    [
+                        jac[b] * half[a][0] + jac[3 + b] * half[a][1] + jac[6 + b] * half[a][2]
+                        for b in range(3)
+                    ]
+                    for a in range(3)
+                ]
+                trace = mu * (full[0][0] + full[1][1] + full[2][2])
+                for c in range(3):
+                    for cp in range(3):
+                        value = mu * full[cp][c] + lam * full[c][cp]
+                        if c == cp:
+                            value = value + trace
+                        start = (p * 3 + cp) * 4 * padded + 32 * i + c
+                        kmat[m, pl.ds(start, 8, stride=4), :] = value
+        return carry
+
+    lax.fori_loop(0, pairs_el, form_stiffness, 0)
 
     rank_row = lax.broadcasted_iota(jnp.int32, (perm.shape[0], LANES), 0)
 
@@ -345,7 +464,7 @@
     for q in range(min(tables, points)):
         build_order(q)
 
-    first = first[:, 0:LANES] + at_nodes(shared_sum(0))
+    first = first + at_nodes(shared_sum(0))
     axis_row = jnp.bitwise_and(row16, 3) < 3
     source = jnp.where(axis_row, first, 0.0)
     total = jnp.concatenate(
@@ -414,32 +533,23 @@
             )
         return tensor
 
-    def internal_force(t):
-        lam = lame_ref[0:1, :]
-        mu = lame_ref[1:2, :]
-        pressure = lam * (t[0][0] + t[1][1] + t[2][2])
-        stress = [[None] * 3 for _ in range(3)]
+    def stiffness(values):
         for c in range(3):
-            for e in range(c, 3):
-                s = mu * (t[c][e] + t[e][c])
-                if c == e:
-                    s = s + pressure
-                stress[c][e] = s
-                stress[e][c] = s
-        weight = pw_ref[...]
-        highs = []
-        lows = []
-        for c in range(3):
-            for r in range(3):
-                m = stress[c][0] * jac_ref[3 * r : 3 * r + 1, :]
-                m = m + stress[c][1] * jac_ref[3 * r + 1 : 3 * r + 2, :]
-                m = m + stress[c][2] * jac_ref[3 * r + 2 : 3 * r + 3, :]
-                hi, lo = split(m * weight)
-                highs.append(hi)
-                lows.append(lo)
-        side = jnp.concatenate(highs + lows + highs, axis=0)
-        values = jnp.dot(w2[...], side, preferred_element_type=F32)
-        return scatter(lambda n: values[8 * n : 8 * n + 8, :])
+            for i in range(tiles):
+                start = c * padded + 8 * i
+                at_el[start : start + 8, :] = values[c][i]
+        sums = [None] * pairs_el
+        for n in range(nodes_el):
+            for cp in range(3):
+                here = c_row(cp * padded + n)
+                for j in range(pairs_el):
+                    start = ((n % 2) * 3 + cp) * 4 * padded + 8 * j
+                    term = kmat[n // 2, start : start + 8, :] * here
+                    sums[j] = term if sums[j] is None else sums[j] + term
+        return [pack(x) for x in sums]
+
+    def c_row(i):
+        return jnp.broadcast_to(at_el[i : i + 1, :], (8, LANES))
 
     def record(t, slot_index):
         comps = [
@@ -506,36 +616,37 @@
         def _():
             out_ref[:, h * half : (h + 1) * half, mine(d)] = last
 
+    def launch(t, values, got, displace, velocity, extra):
+        packs = stiffness(values)
+        send_shared(face_forces(packs), lax.rem(t, 2))
+        record(gradient(values), t - 1)
+        if got is not None:
+            change = half_inverse * at_nodes(got)
+            velocity = velocity - change
+            displace = displace - time_step * change
+        velocity = velocity + half_inverse * (wav_ref[t] * source - node_forces(packs))
+        displace = displace + time_step * velocity
+        values = gather(displace)
+        extra(t)
+        return values, displace, velocity
+
     def advance(t, state, extra):
         values, displace, velocity = state
-        slot = lax.rem(t, 2)
-        tensor = gradient(values)
-        inner = internal_force(tensor)
-        send_shared(inner, slot)
-        velocity = velocity + half_inverse * (wav_ref[t] * source - inner[:, 0:LANES])
-        displace = displace + time_step * velocity
-        values = gather(displace)
-        record(tensor, t - 1)
-        extra(t)
-        got = shared_sum(slot)
-        values = corrected(values, got)
-        change = half_inverse * at_nodes(got)
-        return values, displace - time_step * change, velocity - change
-
-    def early(t, state):
-        def extra(t):
-            for i in range(tables):
-                build_order(jnp.minimum(t * tables + i, points - 1))
-
-        return advance(t, state, extra)
-
-    state = (gather(displace), displace, velocity)
-    state = lax.fori_loop(1, half, early, state)
+        got = shared_sum(lax.rem(t - 1, 2))
+        return launch(t, corrected(values, got), got, displace, velocity, extra)
+
+    def order_some(t):
+        for i in range(tables):
+            build_order(jnp.minimum(t * tables + i, points - 1))
+
+    state = launch(jnp.int32(1), gather(displace), None, displace, velocity, order_some)
+    state = lax.fori_loop(2, half, lambda t, held: advance(t, held, order_some), state)
     state = advance(jnp.int32(half), state, lambda t: ship(0))
     state = lax.fori_loop(
         half + 1, steps, lambda t, held: advance(t, held, lambda t: None), state
     )
-    record(gradient(state[0]), jnp.int32(steps - 1))
+    got = shared_sum(lax.rem(jnp.int32(steps - 1), 2))
+    record(gradient(corrected(state[0], got)), jnp.int32(steps - 1))
     ship(1)
     for h in range(2):
         for i in range(1, writers):
@@ -568,6 +679,7 @@
         points = point_weights.shape[0]
         point_count = point_rank.shape[1]
         steps = wavelet.shape[0]
+        padded = -(-nodes_el // 8) * 8
         vmem = pl.BlockSpec(memory_space=pltpu.VMEM)
         smem = pl.BlockSpec(memory_space=pltpu.SMEM)
         hbm = pl.BlockSpec(memory_space=pl.ANY)
@@ -590,11 +702,16 @@
             scratch_shapes=[pltpu.VMEM(a.shape, a.dtype) for a in sharded] * 2
             + [pltpu.SemaphoreType.DMA((len(sharded),))] * 3
             + [
-                pltpu.VMEM((nodes_el * LANES, 2 * LANES), BF16),
-                pltpu.VMEM((nodes_el * 16, LANES), BF16),
+                pltpu.VMEM((nodes_el // 2 * LANES, 2 * LANES), BF16),
+                pltpu.VMEM((nodes_el // 2 * LANES, 2 * LANES), BF16),
+                pltpu.VMEM((nodes_el // 2 * (source_pattern.shape[1] // LANES) * 16, LANES), BF16),
+                pltpu.VMEM((3, padded, LANES), F32),
+                pltpu.VMEM((nodes_el // 2, 18 * padded, LANES), BF16),
+                pltpu.VMEM((LANES, LANES), BF16),
+                pltpu.VMEM((nodes_el // 2, 24 * padded, LANES), F32),
+                pltpu.VMEM((3 * padded, LANES), F32),
                 pltpu.VMEM((point_count, point_count), BF16),
                 pltpu.VMEM((3 * points, 96), BF16),
-                pltpu.VMEM((nodes_el * 8, 27 * points), BF16),
                 pltpu.VMEM((steps * 6 * points, LANES), F32),
                 pltpu.VMEM((steps // 2 * 6, point_count), BF16),
                 pltpu.VMEM((2, writers, 6, steps // 2, point_count // writers), BF16),

time: 63.8 us -> 61 us (0.956)
  Pallas kernels: 61.5 us -> 58.4 us
    pallas_call x1, Pallas kernels: 61.5 us -> 58.4 us  [shards(): pl.pallas_call(functools.partial(kernel, groups, writers, steps, nodes_el...]
where the time goes in v2:
time: 61 us; the launch traced here: 60.1 us
  Pallas kernels  58.4 us (96%)
  local copies, waits for them, and re-layouts  1.77 us (3%)
    pallas_call x1, Pallas kernels, shards(): pl.pallas_call(functools.partial(kernel, groups, writers, steps, nodes_el...  58.4 us
    unnamed x1, local copies, waits for them, and re-layouts  1.77 us

profile of v2, /device:TPU:0, one launch (start us, length us, event | category | flops | bytes accessed | tf_op | source)
XLA Modules:
  0.0 60.1 jit_solution(15628609717298279263)
XLA Ops:
  0.0 58.4 %window.1 = bf16[6,16,2048]{2,1,0:T(8,128)(2,1)} custom-call(s32[20,128]{1,0:T(8,128)} %conn_in.1, s32[1,4,32]{2,1,0:T(4,128)} %faces_in.1, s32[1,4]{1,0:T(1,128)} %nb_in.1, s32[1,2048]{1,0:T(1,128)} %rank_in.1, f32[9,128]{1,0:T(8,128)} %jac_in.1, f32[2,128]{1,0:T(2,128)} %lame_in.1, f32[16,128]{1,0:T(8,128)} %pw_in.1, f32[20,128]{1,0:T(8,128)} %mass_in.1, ...), custom_call_target="tpu_custom_call" | custom-call | tf_op jit(solution)/shard_map/window/pallas_call | solution.py:697
  58.4 1.8 %copy.13 = bf16[16,6,2048]{2,0,1:T(8,128)(2,1)} copy(bf16[16,6,2048]{2,0,1:T(8,128)(2,1)} %bitcast.2) | data formatting | bytes 786432

commit v3 on v2

--- a/solution.py
+++ b/solution.py
@@ -69,10 +69,14 @@
     pww,
     kmat,
     at_el,
-    perm,
     w1,
-    snaps,
-    lhs,
+    snap,
+    spread,
+    route,
+    stage,
+    mixed,
+    pair,
+    pair_in,
     ordered,
     send,
     recv,
@@ -112,13 +116,13 @@
 
     arrays = (
         (conn_in, conn_own, conn_ref),
+        (faces_in, faces_own, faces_ref),
         (mass_in, mass_own, mass_ref),
-        (faces_in, faces_own, faces_ref),
+        (src_in, src_own, src_ref),
         (nb_in, nb_own, nb_ref),
-        (src_in, src_own, src_ref),
+        (pw_in, pw_own, pw_ref),
         (jac_in, jac_own, jac_ref),
         (lame_in, lame_own, lame_ref),
-        (pw_in, pw_own, pw_ref),
         (rank_in, rank_own, rank_ref),
     )
 
@@ -243,7 +247,13 @@
 
     lax.fori_loop(0, pairs_el, clear, 0)
 
-    landed(0, 5)
+    half = steps // 2
+    held = steps * points * 8
+    last_rows = 2 * points * 8
+    stage[held - last_rows : held, :] = jnp.zeros((last_rows, LANES), F32)
+    snap[...] = jnp.zeros_like(snap)
+
+    landed(0, 2)
     faces = faces_ref[0].astype(F32)
     face_row = jnp.concatenate([faces[k : k + 1, :] for k in range(4)], axis=1)
     face_swap = jnp.concatenate([faces[k ^ 1 : (k ^ 1) + 1, :] for k in range(4)], axis=1)
@@ -305,6 +315,7 @@
             axis=0,
         )
 
+    landed(2, 5)
     quarter = jnp.right_shift(lax.broadcasted_iota(jnp.int32, (8, LANES), 1), 5)
     nb = nb_ref[...].astype(F32)
     recv_mask = [jnp.where(quarter == k, nb[:, k : k + 1], 0.0) for k in range(4)]
@@ -449,20 +460,14 @@
                         kmat[m, pl.ds(start, 8, stride=4), :] = value
         return carry
 
-    lax.fori_loop(0, pairs_el, form_stiffness, 0)
-
-    rank_row = lax.broadcasted_iota(jnp.int32, (perm.shape[0], LANES), 0)
-
-    def build_order(q):
-        start = pl.multiple_of(q * LANES, LANES)
-        perm[:, pl.ds(start, LANES)] = jnp.where(
-            rank_ref[:, pl.ds(start, LANES)] == rank_row, 1.0, 0.0
-        ).astype(BF16)
-
-    half = steps // 2
-    tables = -(-points // half)
-    for q in range(min(tables, points)):
-        build_order(q)
+    group = 5 if pairs_el % 5 == 0 else 1
+
+    def form_group(i, carry):
+        for k in range(group):
+            form_stiffness(i * group + k, carry)
+        return carry
+
+    lax.fori_loop(0, pairs_el // group, form_group, 0)
 
     first = first + at_nodes(shared_sum(0))
     axis_row = jnp.bitwise_and(row16, 3) < 3
@@ -489,24 +494,10 @@
             out.append(acc)
         return out
 
-    inv_f = inv_idx.astype(F32)
-    place = [x.astype(jnp.int32) for x in at_elements(lambda b: inv_f[4 * b : 4 * b + 1, :])]
-    coef = (-time_step) * half_inverse * inv_has
-    coef = at_elements(lambda b: coef[4 * b : 4 * b + 1, :])
-
     def gather(u):
         return tuple(
             tuple(at_elements(lambda b: u[4 * b + c : 4 * b + c + 1, :])) for c in range(3)
         )
-
-    def corrected(values, got):
-        out = []
-        for c in range(3):
-            row = jnp.broadcast_to(got[c : c + 1, :], (8, LANES))
-            out.append(
-                tuple(values[c][i] + pick_lanes(row, place[i]) * coef[i] for i in range(3))
-            )
-        return tuple(out)
 
     def gradient(values):
         sides = []
@@ -551,7 +542,7 @@
     def c_row(i):
         return jnp.broadcast_to(at_el[i : i + 1, :], (8, LANES))
 
-    def record(t, slot_index):
+    def record(t):
         comps = [
             t[0][0],
             t[1][1],
@@ -561,29 +552,60 @@
             0.5 * (t[0][1] + t[1][0]),
         ]
         for c, value in enumerate(comps):
-            start = (slot_index // half) * 6 + c
-            start = pl.multiple_of((start * half + lax.rem(slot_index, half)) * points, points)
-            snaps[pl.ds(start, points), :] = value
+            snap[pl.ds(c, points, stride=8), :] = value
+
+    def build_route():
+        ranks = jnp.concatenate(
+            [rank_ref[:, q * LANES : (q + 1) * LANES] for q in range(points)], axis=0
+        )
+        turned = jnp.concatenate(
+            [ranks.astype(F32), jnp.zeros((LANES - points, LANES), F32)], axis=0
+        ).T.astype(jnp.int32)
+        upper = jnp.right_shift(ranks, 7)
+        place_row = lax.broadcasted_iota(jnp.int32, (points, LANES), 0)
+        lane_value = lax.broadcasted_iota(jnp.int32, (points, LANES), 1).astype(F32)
+        sides = []
+        for q in range(points):
+            low = jnp.broadcast_to(turned[:, q : q + 1], (LANES, LANES))
+            low = jnp.bitwise_and(low, LANES - 1)
+            spread[q * LANES : (q + 1) * LANES, :] = jnp.where(low == lane, 1.0, 0.0).astype(BF16)
+            mine_here = place_row == jnp.broadcast_to(upper[q : q + 1, :], (points, LANES))
+            sides.append(
+                jnp.concatenate(
+                    [jnp.where(mine_here, float(q), 0.0), jnp.where(mine_here, lane_value, 0.0)],
+                    axis=0,
+                ).astype(BF16)
+            )
+        route[...] = jnp.dot(
+            jnp.concatenate(sides, axis=1), spread[...], preferred_element_type=F32
+        ).astype(jnp.int32)
+
+    def in_order():
+        sources = [snap[8 * q : 8 * q + 8, :] for q in range(points)]
+        out = []
+        for k in range(points):
+            origin = jnp.broadcast_to(route[k : k + 1, :], (8, LANES))
+            at = jnp.broadcast_to(route[points + k : points + k + 1, :], (8, LANES))
+            value = pick_lanes(sources[0], at)
+            for q in range(1, points):
+                value = jnp.where(origin == q, pick_lanes(sources[q], at), value)
+            out.append(value)
+        return out
+
+    def keep(t):
+        for k, value in enumerate(in_order()):
+            start = pl.multiple_of(t * (points * 8) + 8 * k, 8)
+            stage[pl.ds(start, 8), :] = value
 
     velocity = wav_ref[0] * source * half_inverse
     displace = time_step * velocity
 
-    def order_for(w):
-        start = pl.multiple_of(w * block, block)
-        res = lax.dot_general(
-            lhs[...],
-            perm[pl.ds(start, block), :],
-            (((1,), (1,)), ((), ())),
-            preferred_element_type=F32,
-        )
-        return res.astype(BF16).reshape(6, half, block)
-
     def mine(i):
         return pl.ds(pl.multiple_of(i * block, block), block)
 
     def parcel(h, i, column, target):
         return pltpu.make_async_remote_copy(
-            src_ref=ordered.at[h, i],
+            src_ref=ordered.at[h, :, :, mine(target)],
             dst_ref=out_ref.at[:, h * half : (h + 1) * half, mine(column)],
             send_sem=out_send_sem.at[h, i],
             recv_sem=out_recv_sem.at[h, i],
@@ -591,35 +613,71 @@
             device_id_type=MESH,
         )
 
-    def arriving(h, i):
-        origin = lax.rem(my_d - i + writers, writers)
-        return parcel(h, i, along(origin), origin)
-
-    def ship(h):
-        count = 6 * half
-        for q in range(points):
-            lhs[:, q * LANES : (q + 1) * LANES] = snaps[
-                pl.ds(h * count * points + q, count, stride=points), :
-            ].astype(BF16)
+    def last_parcel(i, column, target):
+        return pltpu.make_async_remote_copy(
+            src_ref=pair.at[:, mine(target)],
+            dst_ref=pair_in.at[:, mine(column)],
+            send_sem=out_send_sem.at[2, i],
+            recv_sem=out_recv_sem.at[2, i],
+            device_id=(g, target),
+            device_id_type=MESH,
+        )
+
+    def dispatch(make, local):
         for i in range(1, writers):
-            w = lax.rem(my_d + i, writers)
-            ordered[h, i] = order_for(w)
-            parcel(h, i, d, w).start()
-        last = order_for(my_d)
+            make(i, d, lax.rem(my_d + i, writers)).start()
 
         @pl.when(other_core)
         def _():
-            ordered[h, 0] = last
-            parcel(h, 0, d, my_d).start()
-
-        @pl.when(jnp.logical_not(other_core))
+            make(0, d, my_d).start()
+
+        pl.when(jnp.logical_not(other_core))(local)
+
+    def collect(make):
+        for i in range(1, writers):
+            origin = lax.rem(my_d - i + writers, writers)
+            make(i, along(origin), origin).wait_recv()
+            make(i, d, lax.rem(my_d + i, writers)).wait_send()
+
+        @pl.when(other_core)
         def _():
-            out_ref[:, h * half : (h + 1) * half, mine(d)] = last
+            make(0, d, my_d).wait_recv()
+            make(0, d, my_d).wait_send()
+
+    def ship(h):
+        for k in range(points):
+            for c in range(6):
+                start = h * half * points * 8 + 8 * k + c
+                ordered[h, c, :, k * LANES : (k + 1) * LANES] = stage[
+                    pl.ds(start, half, stride=points * 8), :
+                ].astype(BF16)
+
+        def local():
+            out_ref[:, h * half : (h + 1) * half, mine(d)] = ordered[h, :, :, mine(my_d)]
+
+        dispatch(functools.partial(parcel, h), local)
+
+    def finish():
+        for k, value in enumerate(in_order()):
+            start = held - last_rows + 8 * k
+            mixed[k, pl.ds(0, 8, stride=2), :] = stage[start : start + 8, :]
+            mixed[k, pl.ds(1, 8, stride=2), :] = value
+            pair[:, k * LANES : (k + 1) * LANES] = mixed[k].astype(BF16)
+
+        def local():
+            pair_in[:, mine(d)] = pair[:, mine(my_d)]
+
+        dispatch(last_parcel, local)
+        for h in range(2):
+            collect(functools.partial(parcel, h))
+        collect(last_parcel)
+        for c in range(6):
+            out_ref[c, steps - 2 : steps, :] = pair_in[2 * c : 2 * c + 2, :]
 
     def launch(t, values, got, displace, velocity, extra):
         packs = stiffness(values)
         send_shared(face_forces(packs), lax.rem(t, 2))
-        record(gradient(values), t - 1)
+        record(gradient(values))
         if got is not None:
             change = half_inverse * at_nodes(got)
             velocity = velocity - change
@@ -627,36 +685,42 @@
         velocity = velocity + half_inverse * (wav_ref[t] * source - node_forces(packs))
         displace = displace + time_step * velocity
         values = gather(displace)
-        extra(t)
+        extra()
+        keep(t - 1)
         return values, displace, velocity
 
-    def advance(t, state, extra):
+    state = launch(jnp.int32(1), gather(displace), None, displace, velocity, build_route)
+
+    inv_f = inv_idx.astype(F32)
+    place = [x.astype(jnp.int32) for x in at_elements(lambda b: inv_f[4 * b : 4 * b + 1, :])]
+    coef = (-time_step) * half_inverse * inv_has
+    coef = at_elements(lambda b: coef[4 * b : 4 * b + 1, :])
+
+    def corrected(values, got):
+        out = []
+        for c in range(3):
+            row = jnp.broadcast_to(got[c : c + 1, :], (8, LANES))
+            out.append(
+                tuple(values[c][i] + pick_lanes(row, place[i]) * coef[i] for i in range(3))
+            )
+        return tuple(out)
+
+    def advance(t, state):
         values, displace, velocity = state
         got = shared_sum(lax.rem(t - 1, 2))
-        return launch(t, corrected(values, got), got, displace, velocity, extra)
-
-    def order_some(t):
-        for i in range(tables):
-            build_order(jnp.minimum(t * tables + i, points - 1))
-
-    state = launch(jnp.int32(1), gather(displace), None, displace, velocity, order_some)
-    state = lax.fori_loop(2, half, lambda t, held: advance(t, held, order_some), state)
-    state = advance(jnp.int32(half), state, lambda t: ship(0))
-    state = lax.fori_loop(
-        half + 1, steps, lambda t, held: advance(t, held, lambda t: None), state
-    )
+
+        def ships():
+            for h, when in ((0, half), (1, steps - 2)):
+                pl.when(t == when)(functools.partial(ship, h))
+
+        state = launch(t, corrected(values, got), got, displace, velocity, lambda: None)
+        ships()
+        return state
+
+    state = lax.fori_loop(2, steps, advance, state)
     got = shared_sum(lax.rem(jnp.int32(steps - 1), 2))
-    record(gradient(corrected(state[0], got)), jnp.int32(steps - 1))
-    ship(1)
-    for h in range(2):
-        for i in range(1, writers):
-            arriving(h, i).wait_recv()
-            parcel(h, i, d, lax.rem(my_d + i, writers)).wait_send()
-
-        @pl.when(other_core)
-        def _():
-            arriving(h, 0).wait_recv()
-            parcel(h, 0, d, my_d).wait_send()
+    record(gradient(corrected(state[0], got)))
+    finish()
 
 
 def solution(mesh):
@@ -710,17 +774,21 @@
                 pltpu.VMEM((LANES, LANES), BF16),
                 pltpu.VMEM((nodes_el // 2, 24 * padded, LANES), F32),
                 pltpu.VMEM((3 * padded, LANES), F32),
-                pltpu.VMEM((point_count, point_count), BF16),
                 pltpu.VMEM((3 * points, 96), BF16),
-                pltpu.VMEM((steps * 6 * points, LANES), F32),
-                pltpu.VMEM((steps // 2 * 6, point_count), BF16),
-                pltpu.VMEM((2, writers, 6, steps // 2, point_count // writers), BF16),
+                pltpu.VMEM((8 * points, LANES), F32),
+                pltpu.VMEM((points * LANES, LANES), BF16),
+                pltpu.VMEM((2 * points, LANES), jnp.int32),
+                pltpu.VMEM((steps * 8 * points, LANES), F32),
+                pltpu.VMEM((points, 16, LANES), F32),
+                pltpu.VMEM((16, point_count), BF16),
+                pltpu.VMEM((16, point_count), BF16),
+                pltpu.VMEM((2, 6, steps // 2, point_count), BF16),
                 pltpu.VMEM((2, 8, LANES), F32),
                 pltpu.VMEM((2, 4, 8, LANES), F32),
                 pltpu.SemaphoreType.DMA((2, 4)),
                 pltpu.SemaphoreType.DMA((2, 4)),
-                pltpu.SemaphoreType.DMA((2, writers)),
-                pltpu.SemaphoreType.DMA((2, writers)),
+                pltpu.SemaphoreType.DMA((3, writers)),
+                pltpu.SemaphoreType.DMA((3, writers)),
             ],
             compiler_params=pltpu.CompilerParams(
                 collective_id=0, has_side_effects=True, vmem_limit_bytes=56 * 1024 * 1024

time: 61 us -> 57.3 us (0.939)
  Pallas kernels: 58.4 us -> 55 us
    pallas_call x1, Pallas kernels: 58.4 us -> 55 us  [shards(): pl.pallas_call(functools.partial(kernel, groups, writers, steps, nodes_el...]
where the time goes in v3:
time: 57.3 us; the launch traced here: 56.8 us
  Pallas kernels  55 us (96%)
  local copies, waits for them, and re-layouts  1.77 us (3%)
    pallas_call x1, Pallas kernels, shards(): pl.pallas_call(functools.partial(kernel, groups, writers, steps, nodes_el...  55 us
    unnamed x1, local copies, waits for them, and re-layouts  1.77 us

profile of v3, /device:TPU:0, one launch (start us, length us, event | category | flops | bytes accessed | tf_op | source)
XLA Modules:
  0.0 56.8 jit_solution(9192604243846584659)
XLA Ops:
  0.0 55.0 %window.1 = bf16[6,16,2048]{2,1,0:T(8,128)(2,1)} custom-call(s32[20,128]{1,0:T(8,128)} %conn_in.1, s32[1,4,32]{2,1,0:T(4,128)} %faces_in.1, s32[1,4]{1,0:T(1,128)} %nb_in.1, s32[1,2048]{1,0:T(1,128)} %rank_in.1, f32[9,128]{1,0:T(8,128)} %jac_in.1, f32[2,128]{1,0:T(2,128)} %lame_in.1, f32[16,128]{1,0:T(8,128)} %pw_in.1, f32[20,128]{1,0:T(8,128)} %mass_in.1, ...), custom_call_target="tpu_custom_call" | custom-call | tf_op jit(solution)/shard_map/window/pallas_call | solution.py:761
  55.0 1.8 %copy.13 = bf16[16,6,2048]{2,0,1:T(8,128)(2,1)} copy(bf16[16,6,2048]{2,0,1:T(8,128)(2,1)} %bitcast.2) | data formatting | bytes 786432

commit v4 on v3

--- a/solution.py
+++ b/solution.py
@@ -73,11 +73,9 @@
     snap,
     spread,
     route,
-    stage,
     mixed,
     pair,
     pair_in,
-    ordered,
     send,
     recv,
     send_sem,
@@ -141,37 +139,40 @@
             device_id_type=MESH,
         )
 
+    recv[...] = jnp.zeros_like(recv)
+    barrier = pltpu.get_barrier_semaphore()
+
+    @pl.when(moves)
+    def _():
+        pl.semaphore_signal(barrier, inc=1, device_id=(g, d), device_id_type=MESH)
+
+    for k in range(4):
+
+        @pl.when(has[k])
+        def _():
+            pl.semaphore_signal(barrier, inc=1, device_id=where_to[k], device_id_type=MESH)
+
+    for i in range(writers):
+        origin_d = lax.rem(my_d + i, writers)
+        origin = (across(my_g, along(origin_d)), origin_d)
+
+        def greet():
+            pl.semaphore_signal(barrier, inc=1, device_id=origin, device_id_type=MESH)
+
+        if i:
+            greet()
+        else:
+            pl.when(other_core)(greet)
+
     @pl.when(stays)
     def _():
         for i in range(len(arrays)):
             fetch(i, True).start()
 
-    recv[...] = jnp.zeros_like(recv)
-    barrier = pltpu.get_barrier_semaphore()
-
     @pl.when(moves)
     def _():
         for i in range(len(arrays)):
             fetch(i, False).start()
-        pl.semaphore_signal(barrier, inc=1, device_id=(g, d), device_id_type=MESH)
-
-    for k in range(4):
-
-        @pl.when(has[k])
-        def _():
-            pl.semaphore_signal(barrier, inc=1, device_id=where_to[k], device_id_type=MESH)
-
-    for i in range(writers):
-        origin_d = lax.rem(my_d + i, writers)
-        origin = (across(my_g, along(origin_d)), origin_d)
-
-        def greet():
-            pl.semaphore_signal(barrier, inc=1, device_id=origin, device_id_type=MESH)
-
-        if i:
-            greet()
-        else:
-            pl.when(other_core)(greet)
 
     expected = moves.astype(jnp.int32) + other_core.astype(jnp.int32) + writers - 1
     for k in range(4):
@@ -247,10 +248,7 @@
 
     lax.fori_loop(0, pairs_el, clear, 0)
 
-    half = steps // 2
-    held = steps * points * 8
-    last_rows = 2 * points * 8
-    stage[held - last_rows : held, :] = jnp.zeros((last_rows, LANES), F32)
+    chunks = steps // 2
     snap[...] = jnp.zeros_like(snap)
 
     landed(0, 2)
@@ -592,10 +590,9 @@
             out.append(value)
         return out
 
-    def keep(t):
+    def keep(parity):
         for k, value in enumerate(in_order()):
-            start = pl.multiple_of(t * (points * 8) + 8 * k, 8)
-            stage[pl.ds(start, 8), :] = value
+            mixed[k, pl.ds(parity, 8, stride=2), :] = value
 
     velocity = wav_ref[0] * source * half_inverse
     displace = time_step * velocity
@@ -603,22 +600,12 @@
     def mine(i):
         return pl.ds(pl.multiple_of(i * block, block), block)
 
-    def parcel(h, i, column, target):
+    def parcel(chunk, i, column, target):
         return pltpu.make_async_remote_copy(
-            src_ref=ordered.at[h, :, :, mine(target)],
-            dst_ref=out_ref.at[:, h * half : (h + 1) * half, mine(column)],
-            send_sem=out_send_sem.at[h, i],
-            recv_sem=out_recv_sem.at[h, i],
-            device_id=(g, target),
-            device_id_type=MESH,
-        )
-
-    def last_parcel(i, column, target):
-        return pltpu.make_async_remote_copy(
-            src_ref=pair.at[:, mine(target)],
-            dst_ref=pair_in.at[:, mine(column)],
-            send_sem=out_send_sem.at[2, i],
-            recv_sem=out_recv_sem.at[2, i],
+            src_ref=pair.at[chunk, :, mine(target)],
+            dst_ref=pair_in.at[chunk, :, mine(column)],
+            send_sem=out_send_sem.at[chunk, i],
+            recv_sem=out_recv_sem.at[chunk, i],
             device_id=(g, target),
             device_id_type=MESH,
         )
@@ -644,39 +631,23 @@
             make(0, d, my_d).wait_recv()
             make(0, d, my_d).wait_send()
 
-    def ship(h):
+    def send_pair(chunk):
         for k in range(points):
-            for c in range(6):
-                start = h * half * points * 8 + 8 * k + c
-                ordered[h, c, :, k * LANES : (k + 1) * LANES] = stage[
-                    pl.ds(start, half, stride=points * 8), :
-                ].astype(BF16)
+            pair[chunk, :, k * LANES : (k + 1) * LANES] = mixed[k].astype(BF16)
 
         def local():
-            out_ref[:, h * half : (h + 1) * half, mine(d)] = ordered[h, :, :, mine(my_d)]
-
-        dispatch(functools.partial(parcel, h), local)
-
-    def finish():
-        for k, value in enumerate(in_order()):
-            start = held - last_rows + 8 * k
-            mixed[k, pl.ds(0, 8, stride=2), :] = stage[start : start + 8, :]
-            mixed[k, pl.ds(1, 8, stride=2), :] = value
-            pair[:, k * LANES : (k + 1) * LANES] = mixed[k].astype(BF16)
-
-        def local():
-            pair_in[:, mine(d)] = pair[:, mine(my_d)]
-
-        dispatch(last_parcel, local)
-        for h in range(2):
-            collect(functools.partial(parcel, h))
-        collect(last_parcel)
+            pair_in[chunk, :, mine(d)] = pair[chunk, :, mine(my_d)]
+
+        dispatch(functools.partial(parcel, chunk), local)
+
+    def merge(chunk):
+        collect(functools.partial(parcel, chunk))
         for c in range(6):
-            out_ref[c, steps - 2 : steps, :] = pair_in[2 * c : 2 * c + 2, :]
-
-    def launch(t, values, got, displace, velocity, extra):
+            out_ref[c, 2 * chunk : 2 * chunk + 2, :] = pair_in[chunk, 2 * c : 2 * c + 2, :]
+
+    def launch(t, odd, values, got, displace, velocity, extra):
         packs = stiffness(values)
-        send_shared(face_forces(packs), lax.rem(t, 2))
+        send_shared(face_forces(packs), odd)
         record(gradient(values))
         if got is not None:
             change = half_inverse * at_nodes(got)
@@ -686,10 +657,10 @@
         displace = displace + time_step * velocity
         values = gather(displace)
         extra()
-        keep(t - 1)
+        keep(1 - odd)
         return values, displace, velocity
 
-    state = launch(jnp.int32(1), gather(displace), None, displace, velocity, build_route)
+    state = launch(1, 1, gather(displace), None, displace, velocity, build_route)
 
     inv_f = inv_idx.astype(F32)
     place = [x.astype(jnp.int32) for x in at_elements(lambda b: inv_f[4 * b : 4 * b + 1, :])]
@@ -705,22 +676,25 @@
             )
         return tuple(out)
 
-    def advance(t, state):
+    def advance(t, odd, state):
         values, displace, velocity = state
-        got = shared_sum(lax.rem(t - 1, 2))
-
-        def ships():
-            for h, when in ((0, half), (1, steps - 2)):
-                pl.when(t == when)(functools.partial(ship, h))
-
-        state = launch(t, corrected(values, got), got, displace, velocity, lambda: None)
-        ships()
-        return state
-
-    state = lax.fori_loop(2, steps, advance, state)
-    got = shared_sum(lax.rem(jnp.int32(steps - 1), 2))
+        got = shared_sum(1 - odd)
+        return launch(t, odd, corrected(values, got), got, displace, velocity, lambda: None)
+
+    def two_steps(i, state):
+        state = advance(2 * i, 0, state)
+        send_pair(i - 1)
+        return advance(2 * i + 1, 1, state)
+
+    state = lax.fori_loop(1, chunks, two_steps, state)
+    for chunk in range(chunks - 2):
+        merge(chunk)
+    got = shared_sum(1)
     record(gradient(corrected(state[0], got)))
-    finish()
+    keep(1)
+    send_pair(chunks - 1)
+    merge(chunks - 2)
+    merge(chunks - 1)
 
 
 def solution(mesh):
@@ -760,7 +734,7 @@
         )
         ordered = pl.pallas_call(
             functools.partial(kernel, groups, writers, steps, nodes_el),
-            out_shape=jax.ShapeDtypeStruct((6, steps, point_count), BF16),
+            out_shape=pltpu.VMEM((6, steps, point_count), BF16),
             in_specs=[hbm] * len(sharded) + [vmem, smem],
             out_specs=vmem,
             scratch_shapes=[pltpu.VMEM(a.shape, a.dtype) for a in sharded] * 2
@@ -778,17 +752,15 @@
                 pltpu.VMEM((8 * points, LANES), F32),
                 pltpu.VMEM((points * LANES, LANES), BF16),
                 pltpu.VMEM((2 * points, LANES), jnp.int32),
-                pltpu.VMEM((steps * 8 * points, LANES), F32),
                 pltpu.VMEM((points, 16, LANES), F32),
-                pltpu.VMEM((16, point_count), BF16),
-                pltpu.VMEM((16, point_count), BF16),
-                pltpu.VMEM((2, 6, steps // 2, point_count), BF16),
+                pltpu.VMEM((steps // 2, 16, point_count), BF16),
+                pltpu.VMEM((steps // 2, 16, point_count), BF16),
                 pltpu.VMEM((2, 8, LANES), F32),
                 pltpu.VMEM((2, 4, 8, LANES), F32),
                 pltpu.SemaphoreType.DMA((2, 4)),
                 pltpu.SemaphoreType.DMA((2, 4)),
-                pltpu.SemaphoreType.DMA((3, writers)),
-                pltpu.SemaphoreType.DMA((3, writers)),
+                pltpu.SemaphoreType.DMA((steps // 2, writers)),
+                pltpu.SemaphoreType.DMA((steps // 2, writers)),
             ],
             compiler_params=pltpu.CompilerParams(
                 collective_id=0, has_side_effects=True, vmem_limit_bytes=56 * 1024 * 1024

time: 57.3 us -> 56.7 us (0.990)
  local copies, waits for them, and re-layouts: 1.77 us -> 0.75 us
  Pallas kernels: 55 us -> 55.7 us
    unnamed x1, local copies, waits for them, and re-layouts: 1.77 us -> 0.75 us
    pallas_call x1, Pallas kernels: 55 us -> 55.7 us  [shards(): pl.pallas_call(functools.partial(kernel, groups, writers, steps, nodes_el...]
where the time goes in v4:
time: 56.7 us; the launch traced here: 56.5 us
  Pallas kernels  55.7 us (98%)
  local copies, waits for them, and re-layouts  0.75 us (1%)
    pallas_call x1, Pallas kernels, shards(): pl.pallas_call(functools.partial(kernel, groups, writers, steps, nodes_el...  55.7 us

profile of v4, /device:TPU:0, one launch (start us, length us, event | category | flops | bytes accessed | tf_op | source)
XLA Modules:
  0.0 56.5 jit_solution(6513988183248046722)
XLA Ops:
  0.0 55.7 %window.1 = bf16[6,16,2048]{2,1,0:T(8,128)(2,1)S(1)} custom-call(s32[20,128]{1,0:T(8,128)} %conn_in.1, s32[1,4,32]{2,1,0:T(4,128)} %faces_in.1, s32[1,4]{1,0:T(1,128)} %nb_in.1, s32[1,2048]{1,0:T(1,128)} %rank_in.1, f32[9,128]{1,0:T(8,128)} %jac_in.1, f32[2,128]{1,0:T(2,128)} %lame_in.1, f32[16,128]{1,0:T(8,128)} %pw_in.1, f32[20,128]{1,0:T(8,128)} %mass_in.1, ...), custom_call_target="tpu_custom_call" | custom-call | tf_op jit(solution)/shard_map/window/pallas_call | solution.py:735
  55.8 0.7 %copy.13 = bf16[16,6,2048]{2,0,1:T(8,128)(2,1)} copy(bf16[16,6,2048]{2,0,1:T(8,128)(2,1)S(1)} %bitcast.2) | data formatting | bytes 786432

commit v5 on v4

--- a/solution.py
+++ b/solution.py
@@ -37,8 +37,8 @@
     pw_in,
     mass_in,
     src_in,
-    gradt_ref,
-    wav_ref,
+    gradt_in,
+    wav_in,
     out_ref,
     conn_ref,
     faces_ref,
@@ -58,6 +58,8 @@
     pw_own,
     mass_own,
     src_own,
+    gradt_ref,
+    wav_ref,
     move_sem,
     move_send_sem,
     move_recv_sem,
@@ -141,6 +143,10 @@
 
     recv[...] = jnp.zeros_like(recv)
     barrier = pltpu.get_barrier_semaphore()
+    shared = (
+        pltpu.make_async_copy(gradt_in, gradt_ref, move_sem.at[len(arrays)]),
+        pltpu.make_async_copy(wav_in, wav_ref, move_sem.at[len(arrays) + 1]),
+    )
 
     @pl.when(moves)
     def _():
@@ -152,7 +158,8 @@
         def _():
             pl.semaphore_signal(barrier, inc=1, device_id=where_to[k], device_id_type=MESH)
 
-    for i in range(writers):
+    near = writers <= 4
+    for i in range(0 if near else writers):
         origin_d = lax.rem(my_d + i, writers)
         origin = (across(my_g, along(origin_d)), origin_d)
 
@@ -174,7 +181,11 @@
         for i in range(len(arrays)):
             fetch(i, False).start()
 
-    expected = moves.astype(jnp.int32) + other_core.astype(jnp.int32) + writers - 1
+    for copy in shared:
+        copy.start()
+    expected = moves.astype(jnp.int32)
+    if not near:
+        expected = expected + other_core.astype(jnp.int32) + writers - 1
     for k in range(4):
         expected = expected + has[k].astype(jnp.int32)
     pl.semaphore_wait(barrier, expected)
@@ -205,6 +216,8 @@
     padded = -(-nodes_el // 8) * 8
     tiles = padded // 8
 
+    for copy in shared:
+        copy.wait()
     gradt = gradt_ref[...]
     depth = 3 * points
     hi = gradt.astype(BF16).astype(F32)
@@ -631,10 +644,11 @@
             make(0, d, my_d).wait_recv()
             make(0, d, my_d).wait_send()
 
-    def send_pair(chunk):
+    def close_pair(chunk):
         for k in range(points):
             pair[chunk, :, k * LANES : (k + 1) * LANES] = mixed[k].astype(BF16)
 
+    def send_pair(chunk):
         def local():
             pair_in[chunk, :, mine(d)] = pair[chunk, :, mine(my_d)]
 
@@ -645,9 +659,10 @@
         for c in range(6):
             out_ref[c, 2 * chunk : 2 * chunk + 2, :] = pair_in[chunk, 2 * c : 2 * c + 2, :]
 
-    def launch(t, odd, values, got, displace, velocity, extra):
+    def launch(t, odd, values, got, displace, velocity, early, extra):
         packs = stiffness(values)
         send_shared(face_forces(packs), odd)
+        early()
         record(gradient(values))
         if got is not None:
             change = half_inverse * at_nodes(got)
@@ -660,7 +675,12 @@
         keep(1 - odd)
         return values, displace, velocity
 
-    state = launch(1, 1, gather(displace), None, displace, velocity, build_route)
+    def nothing():
+        return None
+
+    state = launch(
+        1, 1, gather(displace), None, displace, velocity, nothing, build_route
+    )
 
     inv_f = inv_idx.astype(F32)
     place = [x.astype(jnp.int32) for x in at_elements(lambda b: inv_f[4 * b : 4 * b + 1, :])]
@@ -676,22 +696,27 @@
             )
         return tuple(out)
 
-    def advance(t, odd, state):
+    def advance(t, odd, state, early):
         values, displace, velocity = state
         got = shared_sum(1 - odd)
-        return launch(t, odd, corrected(values, got), got, displace, velocity, lambda: None)
+        return launch(t, odd, corrected(values, got), got, displace, velocity, early, nothing)
 
     def two_steps(i, state):
-        state = advance(2 * i, 0, state)
-        send_pair(i - 1)
-        return advance(2 * i + 1, 1, state)
+        def early():
+            pl.when(i >= 2)(lambda: send_pair(i - 2))
+
+        state = advance(2 * i, 0, state, early)
+        close_pair(i - 1)
+        return advance(2 * i + 1, 1, state, nothing)
 
     state = lax.fori_loop(1, chunks, two_steps, state)
+    send_pair(chunks - 2)
     for chunk in range(chunks - 2):
         merge(chunk)
     got = shared_sum(1)
     record(gradient(corrected(state[0], got)))
     keep(1)
+    close_pair(chunks - 1)
     send_pair(chunks - 1)
     merge(chunks - 2)
     merge(chunks - 1)
@@ -719,7 +744,6 @@
         steps = wavelet.shape[0]
         padded = -(-nodes_el // 8) * 8
         vmem = pl.BlockSpec(memory_space=pltpu.VMEM)
-        smem = pl.BlockSpec(memory_space=pltpu.SMEM)
         hbm = pl.BlockSpec(memory_space=pl.ANY)
         sharded = (
             connect,
@@ -735,10 +759,11 @@
         ordered = pl.pallas_call(
             functools.partial(kernel, groups, writers, steps, nodes_el),
             out_shape=pltpu.VMEM((6, steps, point_count), BF16),
-            in_specs=[hbm] * len(sharded) + [vmem, smem],
+            in_specs=[hbm] * (len(sharded) + 2),
             out_specs=vmem,
             scratch_shapes=[pltpu.VMEM(a.shape, a.dtype) for a in sharded] * 2
-            + [pltpu.SemaphoreType.DMA((len(sharded),))] * 3
+            + [pltpu.VMEM(shape_grad.shape[::-1], F32), pltpu.SMEM(wavelet.shape, F32)]
+            + [pltpu.SemaphoreType.DMA((len(sharded) + 2,))] * 3
             + [
                 pltpu.VMEM((nodes_el // 2 * LANES, 2 * LANES), BF16),
                 pltpu.VMEM((nodes_el // 2 * LANES, 2 * LANES), BF16),

time: 56.7 us -> 56 us (0.988)
  Pallas kernels: 55.7 us -> 55.1 us
    pallas_call x1, Pallas kernels: 55.7 us -> 55.1 us  [shards(): pl.pallas_call(functools.partial(kernel, groups, writers, steps, nodes_el...]
where the time goes in v5:
time: 56 us; the launch traced here: 55.8 us
  Pallas kernels  55.1 us (98%)
  local copies, waits for them, and re-layouts  0.75 us (1%)
    pallas_call x1, Pallas kernels, shards(): pl.pallas_call(functools.partial(kernel, groups, writers, steps, nodes_el...  55.1 us

profile of v5, /device:TPU:0, one launch (start us, length us, event | category | flops | bytes accessed | tf_op | source)
XLA Modules:
  0.0 55.8 jit_solution(4627479692359375092)
XLA Ops:
  0.0 55.1 %window.1 = bf16[6,16,2048]{2,1,0:T(8,128)(2,1)S(1)} custom-call(s32[20,128]{1,0:T(8,128)} %conn_in.1, s32[1,4,32]{2,1,0:T(4,128)} %faces_in.1, s32[1,4]{1,0:T(1,128)} %nb_in.1, s32[1,2048]{1,0:T(1,128)} %rank_in.1, f32[9,128]{1,0:T(8,128)} %jac_in.1, f32[2,128]{1,0:T(2,128)} %lame_in.1, f32[16,128]{1,0:T(8,128)} %pw_in.1, f32[20,128]{1,0:T(8,128)} %mass_in.1, ...), custom_call_target="tpu_custom_call" | custom-call | tf_op jit(solution)/shard_map/window/pallas_call | solution.py:759
  55.1 0.7 %copy.13 = bf16[16,6,2048]{2,0,1:T(8,128)(2,1)} copy(bf16[16,6,2048]{2,0,1:T(8,128)(2,1)S(1)} %bitcast.2) | data formatting | bytes 786432

commit v6 on v5

--- a/solution.py
+++ b/solution.py
@@ -591,21 +591,17 @@
             jnp.concatenate(sides, axis=1), spread[...], preferred_element_type=F32
         ).astype(jnp.int32)
 
-    def in_order():
-        sources = [snap[8 * q : 8 * q + 8, :] for q in range(points)]
-        out = []
+    def in_order(k):
+        origin = jnp.broadcast_to(route[pl.ds(k, 1), :], (8, LANES))
+        at = jnp.broadcast_to(route[pl.ds(points + k, 1), :], (8, LANES))
+        value = pick_lanes(snap[0:8, :], at)
+        for q in range(1, points):
+            value = jnp.where(origin == q, pick_lanes(snap[8 * q : 8 * q + 8, :], at), value)
+        return value
+
+    def keep(parity):
         for k in range(points):
-            origin = jnp.broadcast_to(route[k : k + 1, :], (8, LANES))
-            at = jnp.broadcast_to(route[points + k : points + k + 1, :], (8, LANES))
-            value = pick_lanes(sources[0], at)
-            for q in range(1, points):
-                value = jnp.where(origin == q, pick_lanes(sources[q], at), value)
-            out.append(value)
-        return out
-
-    def keep(parity):
-        for k, value in enumerate(in_order()):
-            mixed[k, pl.ds(parity, 8, stride=2), :] = value
+            mixed[k, pl.ds(parity, 8, stride=2), :] = in_order(k)
 
     velocity = wav_ref[0] * source * half_inverse
     displace = time_step * velocity
@@ -654,6 +650,26 @@
 
         dispatch(functools.partial(parcel, chunk), local)
 
+    def send_last(chunk):
+        each = block // LANES
+        for i in [*range(1, writers, 2), *range(2, writers, 2), 0]:
+            w = lax.rem(my_d + i, writers)
+            for k in range(each):
+                at = w * each + k
+                mixed[at, pl.ds(1, 8, stride=2), :] = in_order(at)
+                start = pl.multiple_of(at * LANES, LANES)
+                pair[chunk, :, pl.ds(start, LANES)] = mixed[at].astype(BF16)
+            if i:
+                parcel(chunk, i, d, w).start()
+
+        @pl.when(other_core)
+        def _():
+            parcel(chunk, 0, d, my_d).start()
+
+        @pl.when(jnp.logical_not(other_core))
+        def _():
+            pair_in[chunk, :, mine(d)] = pair[chunk, :, mine(my_d)]
+
     def merge(chunk):
         collect(functools.partial(parcel, chunk))
         for c in range(6):
@@ -662,7 +678,6 @@
     def launch(t, odd, values, got, displace, velocity, early, extra):
         packs = stiffness(values)
         send_shared(face_forces(packs), odd)
-        early()
         record(gradient(values))
         if got is not None:
             change = half_inverse * at_nodes(got)
@@ -672,6 +687,7 @@
         displace = displace + time_step * velocity
         values = gather(displace)
         extra()
+        early()
         keep(1 - odd)
         return values, displace, velocity
 
@@ -715,9 +731,12 @@
         merge(chunk)
     got = shared_sum(1)
     record(gradient(corrected(state[0], got)))
-    keep(1)
-    close_pair(chunks - 1)
-    send_pair(chunks - 1)
+    if block % LANES:
+        keep(1)
+        close_pair(chunks - 1)
+        send_pair(chunks - 1)
+    else:
+        send_last(chunks - 1)
     merge(chunks - 2)
     merge(chunks - 1)
 

time: 56 us -> 55.1 us (0.984)
  Pallas kernels: 55.1 us -> 54.1 us
    pallas_call x1, Pallas kernels: 55.1 us -> 54.1 us  [shards(): pl.pallas_call(functools.partial(kernel, groups, writers, steps, nodes_el...]
where the time goes in v6:
time: 55.1 us; the launch traced here: 54.9 us
  Pallas kernels  54.1 us (98%)
  local copies, waits for them, and re-layouts  0.75 us (1%)
    pallas_call x1, Pallas kernels, shards(): pl.pallas_call(functools.partial(kernel, groups, writers, steps, nodes_el...  54.1 us

profile of v6, /device:TPU:0, one launch (start us, length us, event | category | flops | bytes accessed | tf_op | source)
XLA Modules:
  0.0 54.9 jit_solution(10555519624063598463)
XLA Ops:
  0.0 54.1 %window.1 = bf16[6,16,2048]{2,1,0:T(8,128)(2,1)S(1)} custom-call(s32[20,128]{1,0:T(8,128)} %conn_in.1, s32[1,4,32]{2,1,0:T(4,128)} %faces_in.1, s32[1,4]{1,0:T(1,128)} %nb_in.1, s32[1,2048]{1,0:T(1,128)} %rank_in.1, f32[9,128]{1,0:T(8,128)} %jac_in.1, f32[2,128]{1,0:T(2,128)} %lame_in.1, f32[16,128]{1,0:T(8,128)} %pw_in.1, f32[20,128]{1,0:T(8,128)} %mass_in.1, ...), custom_call_target="tpu_custom_call" | custom-call | tf_op jit(solution)/shard_map/window/pallas_call | solution.py:778
  54.1 0.7 %copy.13 = bf16[16,6,2048]{2,0,1:T(8,128)(2,1)} copy(bf16[16,6,2048]{2,0,1:T(8,128)(2,1)S(1)} %bitcast.2) | data formatting | bytes 786432

commit v7 on v6

--- a/solution.py
+++ b/solution.py
@@ -10,6 +10,7 @@
 MESH = pl.DeviceIdType.MESH
 F32 = jnp.float32
 BF16 = jnp.bfloat16
+F8 = jnp.float8_e4m3fn
 time_step = 0.5
 LANES = 128
 
@@ -284,7 +285,7 @@
         return slice(j * LANES, (j + 1) * LANES), slice(p * LANES, (p + 1) * LANES)
 
     for n in range(nodes_el):
-        at_face[spot(n)] = jnp.where(column(n) == face_swap, 1.0, 0.0).astype(BF16)
+        at_face[spot(n)] = jnp.where(column(n) == face_swap, 1.0, 0.0).astype(F8)
 
     def pack(x):
         high = x.astype(BF16).astype(F32)
@@ -365,13 +366,16 @@
             def _():
                 copy.start()
 
+    def departed(slot):
+        for k, copy in enumerate(copies(slot)):
+            pl.when(has[k])(copy.wait_send)
+
     def shared_sum(slot):
         for k, copy in enumerate(arrivals(slot)):
 
             @pl.when(has[k])
             def _():
                 copy.wait_recv()
-                copy.wait_send()
 
         got = recv[slot, 0] * recv_mask[0]
         for k in range(1, 4):
@@ -678,6 +682,7 @@
     def launch(t, odd, values, got, displace, velocity, early, extra):
         packs = stiffness(values)
         send_shared(face_forces(packs), odd)
+        departed(1 - odd)
         record(gradient(values))
         if got is not None:
             change = half_inverse * at_nodes(got)
@@ -737,6 +742,7 @@
         send_pair(chunks - 1)
     else:
         send_last(chunks - 1)
+    departed(1)
     merge(chunks - 2)
     merge(chunks - 1)
 
@@ -784,7 +790,7 @@
             + [pltpu.VMEM(shape_grad.shape[::-1], F32), pltpu.SMEM(wavelet.shape, F32)]
             + [pltpu.SemaphoreType.DMA((len(sharded) + 2,))] * 3
             + [
-                pltpu.VMEM((nodes_el // 2 * LANES, 2 * LANES), BF16),
+                pltpu.VMEM((nodes_el // 2 * LANES, 2 * LANES), F8),
                 pltpu.VMEM((nodes_el // 2 * LANES, 2 * LANES), BF16),
                 pltpu.VMEM((nodes_el // 2 * (source_pattern.shape[1] // LANES) * 16, LANES), BF16),
                 pltpu.VMEM((3, padded, LANES), F32),

time: 55.1 us -> 54.5 us (0.989)
  Pallas kernels: 54.1 us -> 53.2 us
    pallas_call x1, Pallas kernels: 54.1 us -> 53.2 us  [shards(): pl.pallas_call(functools.partial(kernel, groups, writers, steps, nodes_el...]
where the time goes in v7:
time: 54.5 us; the launch traced here: 53.9 us
  Pallas kernels  53.2 us (98%)
  local copies, waits for them, and re-layouts  0.75 us (1%)
    pallas_call x1, Pallas kernels, shards(): pl.pallas_call(functools.partial(kernel, groups, writers, steps, nodes_el...  53.2 us

profile of v7, /device:TPU:0, one launch (start us, length us, event | category | flops | bytes accessed | tf_op | source)
XLA Modules:
  0.0 53.9 jit_solution(11050603534532525584)
XLA Ops:
  0.0 53.2 %window.1 = bf16[6,16,2048]{2,1,0:T(8,128)(2,1)S(1)} custom-call(s32[20,128]{1,0:T(8,128)} %conn_in.1, s32[1,4,32]{2,1,0:T(4,128)} %faces_in.1, s32[1,4]{1,0:T(1,128)} %nb_in.1, s32[1,2048]{1,0:T(1,128)} %rank_in.1, f32[9,128]{1,0:T(8,128)} %jac_in.1, f32[2,128]{1,0:T(2,128)} %lame_in.1, f32[16,128]{1,0:T(8,128)} %pw_in.1, f32[20,128]{1,0:T(8,128)} %mass_in.1, ...), custom_call_target="tpu_custom_call" | custom-call | tf_op jit(solution)/shard_map/window/pallas_call | solution.py:784
  53.2 0.7 %copy.13 = bf16[16,6,2048]{2,0,1:T(8,128)(2,1)} copy(bf16[16,6,2048]{2,0,1:T(8,128)(2,1)S(1)} %bitcast.2) | data formatting | bytes 786432

commit v8 on v7

--- a/solution.py
+++ b/solution.py
@@ -724,7 +724,13 @@
 
     def two_steps(i, state):
         def early():
-            pl.when(i >= 2)(lambda: send_pair(i - 2))
+            @pl.when((i >= 2) & (lax.rem(chunks - 1 - i, 2) == 0))
+            def _():
+                if chunks % 2:
+                    pl.when(i >= 3)(lambda: send_pair(i - 3))
+                else:
+                    send_pair(i - 3)
+                send_pair(i - 2)
 
         state = advance(2 * i, 0, state, early)
         close_pair(i - 1)

time: 54.5 us -> 53.9 us (0.989)
  no operation moved by 1% of the time
where the time goes in v8:
time: 53.9 us; the launch traced here: 53.7 us
  Pallas kernels  53 us (98%)
  local copies, waits for them, and re-layouts  0.75 us (1%)
    pallas_call x1, Pallas kernels, shards(): pl.pallas_call(functools.partial(kernel, groups, writers, steps, nodes_el...  53 us

profile of v8, /device:TPU:0, one launch (start us, length us, event | category | flops | bytes accessed | tf_op | source)
XLA Modules:
  0.0 53.7 jit_solution(6246766378198416037)
XLA Ops:
  0.0 53.0 %window.1 = bf16[6,16,2048]{2,1,0:T(8,128)(2,1)S(1)} custom-call(s32[20,128]{1,0:T(8,128)} %conn_in.1, s32[1,4,32]{2,1,0:T(4,128)} %faces_in.1, s32[1,4]{1,0:T(1,128)} %nb_in.1, s32[1,2048]{1,0:T(1,128)} %rank_in.1, f32[9,128]{1,0:T(8,128)} %jac_in.1, f32[2,128]{1,0:T(2,128)} %lame_in.1, f32[16,128]{1,0:T(8,128)} %pw_in.1, f32[20,128]{1,0:T(8,128)} %mass_in.1, ...), custom_call_target="tpu_custom_call" | custom-call | tf_op jit(solution)/shard_map/window/pallas_call | solution.py:790
  53.0 0.7 %copy.13 = bf16[16,6,2048]{2,0,1:T(8,128)(2,1)} copy(bf16[16,6,2048]{2,0,1:T(8,128)(2,1)S(1)} %bitcast.2) | data formatting | bytes 786432

commit v9 on v8

--- a/solution.py
+++ b/solution.py
@@ -657,13 +657,15 @@
     def send_last(chunk):
         each = block // LANES
         for i in [*range(1, writers, 2), *range(2, writers, 2), 0]:
+            odd_pair = i % 2 and writers % 2 == 0
+            i = jnp.where(lax.rem(my_d, 2) == 0, writers - i, i) if odd_pair else i
             w = lax.rem(my_d + i, writers)
             for k in range(each):
                 at = w * each + k
                 mixed[at, pl.ds(1, 8, stride=2), :] = in_order(at)
                 start = pl.multiple_of(at * LANES, LANES)
                 pair[chunk, :, pl.ds(start, LANES)] = mixed[at].astype(BF16)
-            if i:
+            if odd_pair or i:
                 parcel(chunk, i, d, w).start()
 
         @pl.when(other_core)

time: 53.9 us -> 53.9 us (level)
  no operation moved by 1% of the time
where the time goes in v9:
time: 53.9 us; the launch traced here: 53.7 us
  Pallas kernels  53 us (98%)
  local copies, waits for them, and re-layouts  0.75 us (1%)
    pallas_call x1, Pallas kernels, shards(): pl.pallas_call(functools.partial(kernel, groups, writers, steps, nodes_el...  53 us

profile of v9, /device:TPU:0, one launch (start us, length us, event | category | flops | bytes accessed | tf_op | source)
XLA Modules:
  0.0 53.7 jit_solution(11496510757290527187)
XLA Ops:
  0.0 53.0 %window.1 = bf16[6,16,2048]{2,1,0:T(8,128)(2,1)S(1)} custom-call(s32[20,128]{1,0:T(8,128)} %conn_in.1, s32[1,4,32]{2,1,0:T(4,128)} %faces_in.1, s32[1,4]{1,0:T(1,128)} %nb_in.1, s32[1,2048]{1,0:T(1,128)} %rank_in.1, f32[9,128]{1,0:T(8,128)} %jac_in.1, f32[2,128]{1,0:T(2,128)} %lame_in.1, f32[16,128]{1,0:T(8,128)} %pw_in.1, f32[20,128]{1,0:T(8,128)} %mass_in.1, ...), custom_call_target="tpu_custom_call" | custom-call | tf_op jit(solution)/shard_map/window/pallas_call | solution.py:792
  53.0 0.7 %copy.13 = bf16[16,6,2048]{2,0,1:T(8,128)(2,1)} copy(bf16[16,6,2048]{2,0,1:T(8,128)(2,1)S(1)} %bitcast.2) | data formatting | bytes 786432
